TPU v7x, 1024 devices: a whole 8x8x8 slice. The times are simulated.
1024 devices in a mesh: replica: 64 (over z, x_hi, core), tp: 16 (over x_lo, y).
Axes of the slice: x: 8 (x_hi: 4, x_lo: 2; x = x_hi * 2 + x_lo), y: 8, z: 8, core: 2. Of those that a mesh axis runs over, the one named last changes fastest.
Arguments:
- token_ids: int32 [1024], replicated, may hold values from 0 to 65535
- embed_table: bfloat16 [65536, 8192], P('replica', 'tp'), may hold values from -6 to 6
- norm_gain: bfloat16 [8192], replicated, may hold values from 0.099609375 to 1.8984375
- w_query: bfloat16 [8192, 4096], P(('replica', 'tp')), may hold values from -0.0625 to 0.0625
- w_keyvalue: bfloat16 [8192, 2, 512], P(('replica', 'tp')), may hold values from -0.0625 to 0.0625
- key_cache: bfloat16 [4096, 1024, 128], P(('replica', 'tp')), may hold values from -360 to 360
- value_cache: bfloat16 [4096, 1024, 128], P(('replica', 'tp')), may hold values from -6 to 6
- cache_lengths: int32 [1024], P('replica'), may hold values from 1 to 1024, as said below
Outputs:
- context: bfloat16 [4096, 1024], P(('replica', 'tp'))
- query_weight_tp: bfloat16 [8192, 4096], P(None, 'tp')
- keyvalue_weight_tp: bfloat16 [8192, 2, 512], P(None, None, 'tp')
Inputs may be any that keep to these rules, and one draw needn't show every extreme that they name: `cache_lengths`: some sequence has exactly 1024 filled slots.
All inputs are finite; a program needn't handle non-finite values.
Results may differ from a plain program's by a relative error of at most 0.019.
The roundings to bfloat16 on the way count: a program that leaves them out, or rounds other values in their place, can miss the bound.
Values may be sent and summed in bfloat16 or wider, within the bound.
A program may use at most 64 MiB of HBM per device.

v0:
```python
import jax
import jax.numpy as jnp
from jax import lax
from jax.sharding import Mesh
from jax.sharding import PartitionSpec as P

TP = ("tp_0", "tp_1")
REPLICA_TP = ("replica", "tp_0", "tp_1")


def joined_along(tiles, dim):
    dims = list(tiles.shape[1:])
    dims[dim] *= tiles.shape[0]
    return jnp.moveaxis(tiles, 0, dim).reshape(dims)


def from_everyone(array, axis):
    peers = lax.axis_size(axis)
    return lax.all_to_all(
        jnp.broadcast_to(array[None], (peers, *array.shape)), axis, 0, 0, tiled=True
    )


def gather_directly(array, axis, dim):
    return joined_along(from_everyone(array, axis), dim)


def in_blocks(array, dim, peers):
    dims = array.shape
    tiles = array.reshape(*dims[:dim], peers, dims[dim] // peers, *dims[dim + 1 :])
    return jnp.moveaxis(tiles, dim, 0)


def turned_blocks(tiles, axes, turns):
    dims = [lax.axis_size(a) for a in axes]
    tiles = tiles.reshape(*dims, *tiles.shape[1:])
    for k in turns:
        tiles = lax.all_to_all(tiles, axes[k], split_axis=k, concat_axis=k, tiled=True)
    return tiles.reshape(-1, *tiles.shape[len(axes) :])


def stepwise_exchange(array, axes, turns, split_dim, concat_dim):
    tiles = in_blocks(array, split_dim, lax.axis_size(axes))
    return joined_along(turned_blocks(tiles, axes, turns), concat_dim)


def in_one_piece(arrays, axis, dim, along):
    widths = [a.shape[along] for a in arrays]
    both = jnp.concatenate(arrays, axis=along)
    out = lax.all_gather(both, axis, axis=dim, tiled=True)
    return tuple(jnp.split(out, [sum(widths[:k]) for k in range(1, len(widths))], axis=along))


def gather_packed(arrays, axis, dims):
    vector = jnp.concatenate([a.reshape(-1) for a in arrays])
    lines, at, finished = (lax.all_gather(vector, axis), 0, [])
    for a, dim in zip(arrays, dims):
        tiles = lines[:, at : at + a.size].reshape(-1, *a.shape)
        finished.append(joined_along(tiles, dim))
        at += a.size
    return tuple(finished)


def attend(query, keys, values, key_new, value_new, lengths):
    scale = query.shape[-1] ** (-0.5)
    scores = jnp.einsum("rgd,rcd->rgc", query, keys, preferred_element_type=jnp.float32) * scale
    position = lax.broadcasted_iota(jnp.int32, scores.shape, 2)
    scores = jnp.where(position < lengths[:, None, None], scores, -jnp.inf)
    own = jnp.einsum("rgd,rd->rg", query, key_new, preferred_element_type=jnp.float32) * scale
    top = jnp.maximum(jnp.max(scores, axis=2), own)
    weights = jnp.exp(scores - top[:, :, None])
    own_weight = jnp.exp(own - top)
    total = jnp.sum(weights, axis=2) + own_weight
    weights = (weights / total[:, :, None]).astype(jnp.bfloat16)
    own_weight = (own_weight / total).astype(jnp.bfloat16)
    context = jnp.einsum("rgc,rcd->rgd", weights, values, preferred_element_type=jnp.float32)
    context = (
        context
        + own_weight.astype(jnp.float32)[:, :, None] * value_new.astype(jnp.float32)[:, None, :]
    )
    return context.astype(jnp.bfloat16)


def per_device(
    token_ids, embed_table, norm_gain, w_query, w_keyvalue, key_cache, value_cache, cache_lengths
):
    replicas = lax.axis_size("replica")
    group_index = lax.axis_index("replica")
    tp_index = lax.axis_index(TP)
    vocab_rows, feature_cols = embed_table.shape
    batch = cache_lengths.shape[0]
    first_id = group_index * vocab_rows
    picked = token_ids - first_id
    columns = lax.broadcasted_iota(jnp.int32, (token_ids.shape[0], vocab_rows), 1)
    onehot = (picked[:, None] == columns).astype(jnp.bfloat16)
    local_rows = jnp.dot(onehot, embed_table, preferred_element_type=jnp.float32).astype(
        jnp.bfloat16
    )
    routed = lax.all_to_all(
        local_rows.reshape(replicas, batch, feature_cols),
        "replica",
        split_axis=0,
        concat_axis=0,
        tiled=True,
    )
    embedded = jnp.sum(routed.astype(jnp.float32), axis=0).astype(jnp.bfloat16)
    whole = gather_directly(embedded, TP, 1)
    values32 = whole.astype(jnp.float32)
    mean_square = jnp.mean(values32 * values32, axis=1, keepdims=True)
    normed = (values32 * lax.rsqrt(mean_square + 1e-05) * norm_gain.astype(jnp.float32)).astype(
        jnp.bfloat16
    )
    width = normed.shape[1]
    query_rows = w_query.reshape(w_query.shape[0], 1, w_query.shape[1])
    query_mid, pair_mid = (
        stepwise_exchange(query_rows, TP, (0, 1), 2, 0),
        stepwise_exchange(w_keyvalue, TP, (0, 1), 2, 0),
    )
    flat_query = query_mid.reshape(query_mid.shape[0], query_mid.shape[2])
    pair_cols = pair_mid.shape[2]
    flat_pair = pair_mid.reshape(pair_mid.shape[0], 2 * pair_cols)
    query_full, pair_full = in_one_piece((flat_query, flat_pair), "replica", 0, 1)
    query_acc = jnp.dot(normed, query_full, preferred_element_type=jnp.float32)
    pair_acc = jnp.dot(normed, pair_full, preferred_element_type=jnp.float32)
    query_local = query_acc.astype(jnp.bfloat16)
    pair_local = pair_acc.astype(jnp.bfloat16).reshape(batch, 2, pair_cols)
    query_heads, pair_heads = gather_packed((query_local, pair_local), TP, (1, 2))
    head_size = key_cache.shape[2]
    kv_heads = pair_heads.shape[2] // head_size
    group = query_heads.shape[1] // (kv_heads * head_size)
    rows_here = key_cache.shape[0]
    first_row = tp_index * rows_here
    query_grouped = (
        query_heads.reshape(batch, kv_heads, group, head_size)
        .transpose(1, 0, 2, 3)
        .reshape(kv_heads * batch, group, head_size)
    )
    key_grouped = (
        pair_heads[:, 0]
        .reshape(batch, kv_heads, head_size)
        .transpose(1, 0, 2)
        .reshape(kv_heads * batch, head_size)
    )
    value_grouped = (
        pair_heads[:, 1]
        .reshape(batch, kv_heads, head_size)
        .transpose(1, 0, 2)
        .reshape(kv_heads * batch, head_size)
    )
    query_mine = lax.dynamic_slice_in_dim(query_grouped, first_row, rows_here, 0)
    key_mine = lax.dynamic_slice_in_dim(key_grouped, first_row, rows_here, 0)
    value_mine = lax.dynamic_slice_in_dim(value_grouped, first_row, rows_here, 0)
    sequence = (first_row + lax.broadcasted_iota(jnp.int32, (rows_here,), 0)) % batch
    matches = sequence[:, None] == lax.broadcasted_iota(jnp.int32, (rows_here, batch), 1)
    row_lengths = jnp.sum(jnp.where(matches, cache_lengths[None, :], 0), axis=1)
    context = attend(query_mine, key_cache, value_cache, key_mine, value_mine, row_lengths)
    context = context.reshape(rows_here, group * head_size)
    return (context, query_full, pair_full.reshape(width, 2, pair_cols))


def solution(mesh):
    finer = Mesh(mesh.devices.reshape(mesh.shape["replica"], 2, 8), ("replica", "tp_0", "tp_1"))
    placed = (
        P(),
        P("replica", TP),
        P(),
        P(REPLICA_TP, None),
        P(REPLICA_TP, None, None),
        P(REPLICA_TP, None, None),
        P(REPLICA_TP, None, None),
        P("replica"),
    )
    return jax.shard_map(
        per_device,
        mesh=finer,
        in_specs=placed,
        out_specs=(P(REPLICA_TP, None), P(None, TP), P(None, None, TP)),
        check_vma=False,
    )
```

profile of v0, /device:TPU:4, one launch (start us, length us, event | category | flops | bytes accessed | tf_op | source)
XLA Modules:
  0.0 228.5 jit_solution(8125503282400690136)
XLA Ops:
  7.2 0.8 copy.60
  8.2 6.4 %all_to_all.30 = bf16[2,2,2048]{2,1,0:T(2,128)(2,1)S(1)} all-to-all(bf16[2,2,2048]{2,1,0:T(2,128)(2,1)S(1)} %reshape.97), channel_id=1, replica_groups=mesh['replica'=64,'tp_0'=2,'tp_1'=8] {'tp_0'}, dimensions={0} | all-to-all | bytes 32768 | tf_op jit(solution)/shard_map/all_to_all | solution.py:38
  14.7 3.3 %all-to-all-start.2 = ((bf16[2,8,8,1,256]{4,2,1,3,0:T(8,128)(2,1)}), bf16[2,8,8,1,256]{4,2,1,3,0:T(8,128)(2,1)S(1)}, u32[]{:S(2)}, u32[]{:S(2)}) async-start(bf16[2,8,8,1,256]{4,2,1,3,0:T(8,128)(2,1)} %bitcast.73), calls=%async_computation.2 | async-start | bytes 131072 | tf_op jit(solution)/shard_map/all_to_all | solution.py:38
  18.1 0.7 reshape.99
  18.9 3.2 %all-to-all-done.2 = bf16[2,8,8,1,256]{4,2,1,3,0:T(8,128)(2,1)S(1)} async-done(((bf16[2,8,8,1,256]{4,2,1,3,0:T(8,128)(2,1)}), bf16[2,8,8,1,256]{4,2,1,3,0:T(8,128)(2,1)S(1)}, u32[]{:S(2)}, u32[]{:S(2)}) %all-to-all-start.2) | async-done | bytes 65568 | tf_op jit(solution)/shard_map/all_to_all | solution.py:38
  22.1 7.6 %all-to-all-start.5 = ((bf16[8,2,512]{2,1,0:T(2,128)(2,1)}), bf16[8,2,512]{2,1,0:T(2,128)(2,1)S(1)}, u32[]{:S(2)}, u32[]{:S(2)}) async-start(bf16[8,2,512]{2,1,0:T(2,128)(2,1)} %reshape.99), calls=%async_computation.5 | async-start | bytes 32768 | tf_op jit(solution)/shard_map/all_to_all | solution.py:38
  30.3 7.1 %all-to-all-done.5 = bf16[8,2,512]{2,1,0:T(2,128)(2,1)S(1)} async-done(((bf16[8,2,512]{2,1,0:T(2,128)(2,1)}), bf16[8,2,512]{2,1,0:T(2,128)(2,1)S(1)}, u32[]{:S(2)}, u32[]{:S(2)}) %all-to-all-start.5) | async-done | bytes 16416 | tf_op jit(solution)/shard_map/all_to_all | solution.py:38
  37.4 3.4 %all-to-all-start.3 = ((bf16[2,8,8,1,256]{4,2,0,3,1:T(8,128)(2,1)}), bf16[2,8,8,1,256]{4,2,0,3,1:T(8,128)(2,1)S(1)}, u32[]{:S(2)}, u32[]{:S(2)}) async-start(bf16[2,8,8,1,256]{4,2,0,3,1:T(8,128)(2,1)} %copy.58), calls=%async_computation.3 | async-start | bytes 131072 | tf_op jit(solution)/shard_map/all_to_all | solution.py:38
  41.1 8.0 %all-to-all-done.3 = bf16[2,8,8,1,256]{4,2,0,3,1:T(8,128)(2,1)S(1)} async-done(((bf16[2,8,8,1,256]{4,2,0,3,1:T(8,128)(2,1)}), bf16[2,8,8,1,256]{4,2,0,3,1:T(8,128)(2,1)S(1)}, u32[]{:S(2)}, u32[]{:S(2)}) %all-to-all-start.3) | async-done | bytes 65568 | tf_op jit(solution)/shard_map/all_to_all | solution.py:38
  50.4 1.3 fusion.2
  51.7 56.9 %all_to_all.31 = bf16[64,16,512]{2,1,0:T(8,128)(2,1)S(1)} all-to-all(bf16[64,16,512]{2,1,0:T(8,128)(2,1)S(1)} %bitcast.60), channel_id=1, replica_groups=mesh['replica'=64,'tp_0'=2,'tp_1'=8] {'replica'}, dimensions={0} | all-to-all | bytes 2097152 | tf_op jit(solution)/shard_map/all_to_all | solution.py:99
  108.8 0.7 broadcast_in_dim.20
  109.5 3.5 %all-to-all-start.1 = ((bf16[16,16,512]{2,1,0:T(8,128)(2,1)}), bf16[16,16,512]{2,1,0:T(8,128)(2,1)S(1)}, u32[]{:S(2)}, u32[]{:S(2)}) async-start(bf16[16,16,512]{2,1,0:T(8,128)(2,1)} %broadcast_in_dim.20), calls=%async_computation.1 | async-start | bytes 524288 | tf_op jit(solution)/shard_map/all_to_all | solution.py:19
  113.1 0.7 select_reduce_fusion
  113.8 10.6 %all-to-all-done.1 = bf16[16,16,512]{2,1,0:T(8,128)(2,1)S(1)} async-done(((bf16[16,16,512]{2,1,0:T(8,128)(2,1)}), bf16[16,16,512]{2,1,0:T(8,128)(2,1)S(1)}, u32[]{:S(2)}, u32[]{:S(2)}) %all-to-all-start.1) | async-done | bytes 262176 | tf_op jit(solution)/shard_map/all_to_all | solution.py:19
  124.7 48.0 %all-gather.3.cloned.1.call-done = bf16[8192,320]{1,0:T(8,128)(2,1)} async-done(((bf16[128,320]{1,0:T(8,128)(2,1)}), bf16[8192,320]{1,0:T(8,128)(2,1)}) %all-gather.3.cloned.1.call-update) | async-done | bytes 5242896 | tf_op jit(solution)/shard_map/all_gather | solution.py:50
  172.6 2.6 %split.8 = bf16[8192,256]{1,0:T(8,128)(2,1)S(1)} slice(bf16[8192,320]{1,0:T(8,128)(2,1)} %all-gather.3.cloned.1.call-done), slice={[0:8192], [0:256]} | slice | bytes 8388608 | tf_op jit(solution)/shard_map/split | solution.py:51
  175.3 2.0 copy-done.1
  177.3 0.7 fusion.6
  178.5 35.3 %all-gather = bf16[81920]{0:T(1024)(128)(2,1)S(1)} all-gather(bf16[5120]{0:T(1024)(128)(2,1)S(1)} %pad_maximum_fusion.1), channel_id=2, replica_groups=mesh['replica'=64,'tp_0'=2,'tp_1'=8] {'tp_0','tp_1'}, dimensions={0}, use_global_device_ids=true | all-gather | bytes 174080 | tf_op jit(solution)/shard_map/all_gather | solution.py:56
  215.2 0.7 dynamic-slice_bitcast_fusion
  216.0 1.7 fusion.22
  217.9 1.5 fusion.5
  220.1 1.6 copy.69
  (57 shorter events, 5.9 us)
Async XLA Ops:
  7.2 43.3 %copy-start = (bf16[1024,512]{1,0:T(8,128)(2,1)S(1)}, bf16[1024,512]{1,0:T(8,128)(2,1)}, u32[]{:S(2)}) copy-start(bf16[1024,512]{1,0:T(8,128)(2,1)} %param.9) | copy-start | bytes 3145732
  14.7 7.4 %all-to-all-start.2 = ((bf16[2,8,8,1,256]{4,2,1,3,0:T(8,128)(2,1)}), bf16[2,8,8,1,256]{4,2,1,3,0:T(8,128)(2,1)S(1)}, u32[]{:S(2)}, u32[]{:S(2)}) async-start(bf16[2,8,8,1,256]{4,2,1,3,0:T(8,128)(2,1)} %bitcast.73), calls=%async_computation.2 | async-start | bytes 131072 | tf_op jit(solution)/shard_map/all_to_all | solution.py:38
  22.1 15.3 %all-to-all-start.5 = ((bf16[8,2,512]{2,1,0:T(2,128)(2,1)}), bf16[8,2,512]{2,1,0:T(2,128)(2,1)S(1)}, u32[]{:S(2)}, u32[]{:S(2)}) async-start(bf16[8,2,512]{2,1,0:T(2,128)(2,1)} %reshape.99), calls=%async_computation.5 | async-start | bytes 32768 | tf_op jit(solution)/shard_map/all_to_all | solution.py:38
  37.4 11.7 %all-to-all-start.3 = ((bf16[2,8,8,1,256]{4,2,0,3,1:T(8,128)(2,1)}), bf16[2,8,8,1,256]{4,2,0,3,1:T(8,128)(2,1)S(1)}, u32[]{:S(2)}, u32[]{:S(2)}) async-start(bf16[2,8,8,1,256]{4,2,0,3,1:T(8,128)(2,1)} %copy.58), calls=%async_computation.3 | async-start | bytes 131072 | tf_op jit(solution)/shard_map/all_to_all | solution.py:38
  40.8 131.9 %all-gather.3.cloned.1.call-start = ((), (), s32[]{:S(2)}) async-start(), calls=%async_computation.6 | async-start | bytes 6389760 | tf_op jit(solution)/shard_map/all_gather | solution.py:50
  50.4 62.6 %copy-start.3 = (bf16[8192]{0:T(1024)(128)(2,1)S(1)}, bf16[8192]{0:T(1024)(128)(2,1)}, u32[]{:S(2)}) copy-start(bf16[8192]{0:T(1024)(128)(2,1)} %param.10) | copy-start | bytes 49156
  50.4 62.6 %copy-start.4 = (s32[16]{0:T(128)S(1)}, s32[16]{0:T(128)}, u32[]{:S(2)}) copy-start(s32[16]{0:T(128)} %param.15) | copy-start | bytes 196
  109.5 14.9 %all-to-all-start.1 = ((bf16[16,16,512]{2,1,0:T(8,128)(2,1)}), bf16[16,16,512]{2,1,0:T(8,128)(2,1)S(1)}, u32[]{:S(2)}, u32[]{:S(2)}) async-start(bf16[16,16,512]{2,1,0:T(8,128)(2,1)} %broadcast_in_dim.20), calls=%async_computation.1 | async-start | bytes 524288 | tf_op jit(solution)/shard_map/all_to_all | solution.py:19
  172.6 5.3 %copy-start.2 = (bf16[8192,320]{1,0:T(8,128)(2,1)S(1)}, bf16[8192,320]{1,0:T(8,128)(2,1)}, u32[]{:S(2)}) copy-start(bf16[8192,320]{1,0:T(8,128)(2,1)} %all-gather.3.cloned.1.call-done) | copy-start | bytes 15728644
  175.2 2.0 copy-start.1
  214.1 6.0 %slice-start = ((bf16[8192,320]{1,0:T(8,128)(2,1)}), bf16[8192,64]{1,0:T(8,128)(2,1)S(1)}, s32[]{:S(2)}) async-start(bf16[8192,320]{1,0:T(8,128)(2,1)} %all-gather.3.cloned.1.call-done), calls=%async_computation.7 | async-start | bytes 4194304 | tf_op jit(solution)/shard_map/split | solution.py:51
Sparse Core Ops, SparseCore 0:
  49.9 122.7 all-gather.2
where the time goes:
time: 229 us
  blocking collectives  98.6 us (43%)
  waiting for transfers between devices  76.9 us (34%)
  starting transfers between devices  17.8 us (8%)
  between operations  14.3 us (6%)
  local copies, waits for them, and re-layouts  12.5 us (5%)
  matrix products  5.78 us (3%)
  other arithmetic  2.7 us (1%)
    all_to_all x1, blocking collectives, per_device(): lax.all_to_all(local_rows.reshape(replicas, batch, feature_cols), 'replic...  56.9 us
    all_gather x1, waiting for transfers between devices, in_one_piece(): out = lax.all_gather(both, axis, axis=dim, tiled=True)  48 us
    all_gather x1, blocking collectives, gather_packed(): lines, at, finished = (lax.all_gather(vector, axis), 0, [])  35.3 us
    all_to_all x3, waiting for transfers between devices, turned_blocks(): lax.all_to_all(tiles, axes[k], split_axis=k, concat_axis=k, tiled=True)  18.3 us
    all_to_all x3, starting transfers between devices, turned_blocks(): lax.all_to_all(tiles, axes[k], split_axis=k, concat_axis=k, tiled=True)  14.2 us
    all_to_all x1, waiting for transfers between devices, from_everyone(): lax.all_to_all(jnp.broadcast_to(array[None], (peers, *array.shape)), axis...  10.6 us
    all_to_all x1, blocking collectives, turned_blocks(): lax.all_to_all(tiles, axes[k], split_axis=k, concat_axis=k, tiled=True)  6.41 us
  transfers between devices with their start and end apart: 5, of which 5 were waited for; matrix products, arithmetic and copies ran while one was open for 2% of the time, Pallas kernels for 0%

commit v1 on v0

v1 whole, which is shorter than its diff:
```python
import functools
import jax
import jax.numpy as jnp
from jax import lax
from jax.experimental import pallas as pl
from jax.experimental.pallas import tpu as pltpu
from jax.sharding import PartitionSpec as P

MESH = pl.DeviceIdType.MESH
Z, XH, CORES, TPS = 8, 4, 2, 16
GROUPS = Z * XH * CORES
BATCH, HEAD, GROUP, KVH = 16, 128, 8, 4
FEAT = 512
ROWS = 128
BLOCK = 160
HALF = BLOCK // 2
QCOLS = 256
KVCOLS = 64
MSG = 384


def ring_events(block_us=1.76, lag_us=2.2, first_us=(0.0, 4.5, 9.0, 4.5)):
    ready = [(first_us[j], 0, j) for j in range(XH)]
    free, events = 0.0, []
    while ready:
        ready.sort()
        at, step, j = ready.pop(0)
        if step == 0:
            events.append((at, 0, j))
        else:
            events.append((at, step, j))
        if step < 4:
            begin = max(free, at)
            free = begin + (block_us if step < 3 else block_us / 2)
            ready.append((free + lag_us, step + 1, j))
    return events


def handoff_kernel(
    msg, part, gain, blocks, mixed,
    pieces, got_core, sums_core, got_x, sums_x, got_z, sums_z, embedded, normed, sent, acc_q, acc_kv,
    p1_s, p1_r, xw_s, xw_r, zp_s, zp_r, zm_s, zm_r, pf_s, pf_r, e1_s, e1_r, e2_s, e2_r, e3_s, e3_r,
    e4_s, e4_r, e7_s, e7_r,
):
    r, t = lax.axis_index("replica"), lax.axis_index("tp")
    z, xh, c = r // 8, (r // 2) % 4, r % 2

    def rep(z_, xh_, c_):
        return (z_ * XH + xh_) * CORES + c_

    def dev(rep_, tp_):
        return {"replica": rep_, "tp": tp_}

    partner = dev(rep(z, xh, 1 - c), t)

    def x_peer(d):
        return dev(rep(z, (xh + d) % XH, c), t)

    def z_peer(d):
        return dev(rep((z + d) % Z, xh, c), t)

    def t_peer(d):
        return dev(r, (t + d) % TPS)

    barrier = pltpu.get_barrier_semaphore()
    peers = [partner] + [x_peer(d) for d in (1, 2, 3)] + [z_peer(d) for d in range(1, 8)]
    peers += [t_peer(d) for d in range(1, 16)]
    for p in peers:
        pl.semaphore_signal(barrier, inc=1, device_id=p, device_id_type=MESH)

    started = []

    def send(src, dst, ss, rs, to):
        copy = pltpu.make_async_remote_copy(
            src_ref=src, dst_ref=dst, send_sem=ss, recv_sem=rs, device_id=to, device_id_type=MESH
        )
        copy.start()
        started.append(copy)

    def arrived(dst, rs, frm):
        pltpu.make_async_remote_copy(
            src_ref=dst, dst_ref=dst, send_sem=rs, recv_sem=rs, device_id=frm, device_id_type=MESH
        ).wait_recv()

    pieces[t] = msg[t]
    pl.semaphore_wait(barrier, len(peers))

    send(part.at[1 - c], got_core, e1_s.at[0], e1_r.at[0], partner)
    for d in range(1, 16):
        send(msg.at[(t + d) % TPS], pieces.at[t], p1_s.at[d], p1_r.at[d], t_peer(d))

    arrived(got_core, e1_r.at[0], partner)

    @pl.loop(0, XH)
    def _(a):
        sums_core[a] = part[c, a] + got_core[a]

    for d in range(1, 16):
        arrived(pieces.at[(t - d + TPS) % TPS], p1_r.at[d], t_peer(d))
    own = rep(z, xh, c)
    blocks[own, 0:ROWS, :] = pieces[:, :, 0:QCOLS].reshape(ROWS, QCOLS)
    turned = pieces[:, :, QCOLS:MSG].reshape(ROWS, HEAD).astype(jnp.float32).T.astype(jnp.bfloat16)
    blocks[own, ROWS:BLOCK, 0:HEAD] = turned[0:32]
    blocks[own, ROWS:BLOCK, HEAD:QCOLS] = turned[32:64]

    def block_id(dz, j):
        return rep((z + dz + 2 * Z) % Z, (xh - j + XH) % XH, c)

    def mirrored(dz, j):
        return rep((z + dz + 2 * Z) % Z, (xh - j + XH) % XH, 1 - c)

    lower, upper = pl.ds(0, HALF), pl.ds(HALF, HALF)

    def to_ring(j, step):
        up, down = blocks.at[block_id(-step, j)], blocks.at[block_id(step, j)]
        if step == 3:
            up, down = up.at[lower], down.at[upper]
        send(up, up, zp_s.at[j, step], zp_r.at[j, step], z_peer(1))
        send(down, down, zm_s.at[j, step], zm_r.at[j, step], z_peer(Z - 1))

    def to_partner(ref, k, j):
        send(ref, ref, pf_s.at[j, k], pf_r.at[j, k], partner)

    def on_block(step, j):
        if step == 0:
            if j:
                arrived(blocks.at[block_id(0, j)], xw_r.at[j], x_peer(XH - j))
            to_ring(j, 0)
            if j == 0:
                for d in (1, 3, 2):
                    send(blocks.at[own], blocks.at[own], xw_s.at[d], xw_r.at[d], x_peer(d))
            to_partner(blocks.at[block_id(0, j)], 0, j)
            return
        up, down = blocks.at[block_id(-step, j)], blocks.at[block_id(step, j)]
        if step == 4:
            up, down = up.at[lower], down.at[upper]
        arrived(up, zp_r.at[j, step - 1], z_peer(Z - 1))
        arrived(down, zm_r.at[j, step - 1], z_peer(1))
        if step < 4:
            to_ring(j, step)
        to_partner(up, 2 * step - 1, j)
        to_partner(down, 2 * step, j)

    def send_x_sums():
        for d in (1, 3, 2):
            send(sums_core.at[(xh + d) % XH], got_x.at[d - 1], e2_s.at[d], e2_r.at[d], x_peer(d))

    def add_x_sums():
        for d in (1, 3, 2):
            arrived(got_x.at[d - 1], e2_r.at[d], x_peer(XH - d))

        @pl.loop(0, Z)
        def _(a):
            sums_x[a] = (sums_core[xh, a] + got_x[0, a]) + (got_x[1, a] + got_x[2, a])

        for d in (4, 3, 5, 2, 6, 1, 7):
            send(sums_x.at[(z + d) % Z], got_z.at[d - 1], e3_s.at[d], e3_r.at[d], z_peer(d))

    def add_z_sums():
        for d in range(1, 8):
            arrived(got_z.at[d - 1], e3_r.at[d], z_peer(Z - d))
        total = sums_x[z]
        for d in range(1, 8):
            total = total + got_z[d - 1]
        sums_z[...] = total
        embedded[t] = total
        for d in (12, 4, 11, 5, 13, 3, 10, 6, 14, 2, 9, 7, 15, 1, 8):
            send(sums_z, embedded.at[t], e4_s.at[d], e4_r.at[d], t_peer(d))

    todo = [(at, 0, functools.partial(on_block, step, j)) for at, step, j in ring_events()]
    todo += [(0.1, 1, send_x_sums), (18.0, 1, add_x_sums), (24.0, 1, add_z_sums)]
    for _, _, act in sorted(todo, key=lambda item: item[:2]):
        act()

    for d in range(1, 16):
        arrived(embedded.at[(t - d + TPS) % TPS], e4_r.at[d], t_peer(d))

    def squares(k, total):
        v = embedded[k].astype(jnp.float32)
        return total + v * v

    squared = lax.fori_loop(0, TPS, squares, jnp.zeros((BATCH, FEAT), jnp.float32))
    mean_square = jnp.sum(squared, axis=1, keepdims=True) * (1.0 / (TPS * FEAT))
    factor = lax.rsqrt(mean_square + 1e-05)

    @pl.loop(0, TPS)
    def _(k):
        normed[k] = (embedded[k].astype(jnp.float32) * factor * gain[k].astype(jnp.float32)).astype(
            jnp.bfloat16
        )

    for j in range(XH):
        arrived(blocks.at[mirrored(0, j)], pf_r.at[j, 0], partner)
        for step in range(1, 5):
            up, down = blocks.at[mirrored(-step, j)], blocks.at[mirrored(step, j)]
            if step == 4:
                up, down = up.at[lower], down.at[upper]
            arrived(up, pf_r.at[j, 2 * step - 1], partner)
            arrived(down, pf_r.at[j, 2 * step], partner)

    acc_q[...] = jnp.zeros_like(acc_q)
    acc_kv[...] = jnp.zeros_like(acc_kv)

    @pl.loop(0, TPS)
    def _(k):
        lhs = normed[k]
        rows = [blocks[4 * k + i, 0:ROWS, :] for i in range(4)]
        acc_q[...] += jnp.dot(
            lhs, jnp.concatenate(rows, axis=0), preferred_element_type=jnp.float32
        )
        keys = [blocks[4 * k + i, ROWS:BLOCK, 0:HEAD] for i in range(4)]
        values = [blocks[4 * k + i, ROWS:BLOCK, HEAD:QCOLS] for i in range(4)]
        both = jnp.concatenate(
            [jnp.concatenate(keys, axis=1), jnp.concatenate(values, axis=1)], axis=0
        )
        acc_kv[:, 0:KVCOLS] += lax.dot_general(
            lhs, both, (((1,), (1,)), ((), ())), preferred_element_type=jnp.float32
        )

    quarter = t % 4
    for i in range(4):
        sent[i, :, 0:QCOLS] = acc_q[4 * i : 4 * i + 4, :].astype(jnp.bfloat16)
        sent[i, :, QCOLS:MSG] = acc_kv[4 * i : 4 * i + 4, :].astype(jnp.bfloat16)
    mixed[quarter] = sent[quarter]
    for d in range(1, 4):
        to = (quarter + d) % 4
        send(sent.at[to], mixed.at[quarter], e7_s.at[d], e7_r.at[d], dev(r, t - quarter + to))
    for d in range(1, 4):
        frm = (quarter - d + 4) % 4
        arrived(mixed.at[frm], e7_r.at[d], dev(r, t - quarter + frm))
    for copy in started:
        copy.wait_send()


def handoff(msg, part, gain):
    bf16, f32 = jnp.bfloat16, jnp.float32
    vmem = pl.BlockSpec(memory_space=pltpu.VMEM)
    dma = pltpu.SemaphoreType.DMA
    return pl.pallas_call(
        handoff_kernel,
        out_shape=(
            jax.ShapeDtypeStruct((GROUPS, BLOCK, QCOLS), bf16),
            jax.ShapeDtypeStruct((4, 4, MSG), bf16),
        ),
        in_specs=[vmem] * 3,
        out_specs=(vmem, vmem),
        scratch_shapes=[
            pltpu.VMEM((TPS, 8, MSG), bf16),
            pltpu.VMEM((XH, Z, BATCH, FEAT), bf16),
            pltpu.VMEM((XH, Z, BATCH, FEAT), bf16),
            pltpu.VMEM((3, Z, BATCH, FEAT), bf16),
            pltpu.VMEM((Z, BATCH, FEAT), bf16),
            pltpu.VMEM((7, BATCH, FEAT), bf16),
            pltpu.VMEM((BATCH, FEAT), bf16),
            pltpu.VMEM((TPS, BATCH, FEAT), bf16),
            pltpu.VMEM((TPS, BATCH, FEAT), bf16),
            pltpu.VMEM((4, 4, MSG), bf16),
            pltpu.VMEM((BATCH, QCOLS), f32),
            pltpu.VMEM((BATCH, HEAD), f32),
            dma((16,)), dma((16,)), dma((4,)), dma((4,)),
            dma((4, 4)), dma((4, 4)), dma((4, 4)), dma((4, 4)),
            dma((4, 9)), dma((4, 9)), dma((1,)), dma((1,)),
            dma((4,)), dma((4,)), dma((8,)), dma((8,)),
            dma((16,)), dma((16,)), dma((4,)), dma((4,)),
        ],
        compiler_params=pltpu.CompilerParams(
            collective_id=0, has_side_effects=True, vmem_limit_bytes=40 << 20
        ),
        cost_estimate=pl.CostEstimate(flops=1 << 34, bytes_accessed=1 << 23, transcendentals=0),
        name="handoff",
    )(msg, part, gain)


def attend_kernel(
    lengths, mixed, blocks, keys_hbm, values_hbm, context, query_out, pair_out, keys, values, pair, sems
):
    copies = [
        pltpu.make_async_copy(keys_hbm, keys, sems.at[0]),
        pltpu.make_async_copy(values_hbm, values, sems.at[1]),
        pltpu.make_async_copy(blocks.at[:, 0:ROWS, :], query_out, sems.at[2]),
    ]
    for copy in copies:
        copy.start()

    for g in range(GROUPS):
        pair[0:32, g * ROWS : (g + 1) * ROWS] = blocks[g, ROWS:BLOCK, 0:HEAD]
        pair[32:64, g * ROWS : (g + 1) * ROWS] = blocks[g, ROWS:BLOCK, HEAD:QCOLS]
    last = pltpu.make_async_copy(pair, pair_out, sems.at[3])
    last.start()
    got = [mixed[j].astype(jnp.float32) for j in range(4)]
    scale = HEAD ** (-0.5)
    copies[0].wait()
    rows = []
    for r in range(4):
        heads = [got[j][r : r + 1, k * HEAD : (k + 1) * HEAD] for j in range(4) for k in range(2)]
        query32 = jnp.concatenate(heads, axis=0)
        query = query32.astype(jnp.bfloat16)
        key_new = jnp.concatenate([got[j][r : r + 1, QCOLS : QCOLS + 32] for j in range(4)], axis=1)
        value_new = jnp.concatenate(
            [got[j][r : r + 1, QCOLS + 32 : QCOLS + 64] for j in range(4)], axis=1
        )
        scores = (
            lax.dot_general(
                query, keys[r], (((1,), (1,)), ((), ())), preferred_element_type=jnp.float32
            )
            * scale
        )
        position = lax.broadcasted_iota(jnp.int32, scores.shape, 1)
        scores = jnp.where(position < lengths[r], scores, -jnp.inf)
        own = jnp.sum(query32 * key_new, axis=1, keepdims=True) * scale
        top = jnp.maximum(jnp.max(scores, axis=1, keepdims=True), own)
        weights = jnp.exp(scores - top)
        own_weight = jnp.exp(own - top)
        total = jnp.sum(weights, axis=1, keepdims=True) + own_weight
        weights = (weights / total).astype(jnp.bfloat16)
        own_weight = (own_weight / total).astype(jnp.bfloat16).astype(jnp.float32)
        if r == 0:
            copies[1].wait()
        found = jnp.dot(weights, values[r], preferred_element_type=jnp.float32)
        rows.append(found + own_weight * value_new)
    lanes = [jnp.concatenate([rows[r][h : h + 1] for r in range(4)], axis=0) for h in range(GROUP)]
    context[...] = jnp.concatenate(lanes, axis=1).astype(jnp.bfloat16)
    copies[2].wait()
    last.wait()


def attend(lengths, mixed, blocks, keys, values):
    bf16 = jnp.bfloat16
    vmem = pl.BlockSpec(memory_space=pltpu.VMEM)
    anywhere = pl.BlockSpec(memory_space=pl.ANY)
    hbm = pl.BlockSpec(memory_space=pltpu.HBM)
    return pl.pallas_call(
        attend_kernel,
        out_shape=(
            jax.ShapeDtypeStruct((4, GROUP * HEAD), bf16),
            jax.ShapeDtypeStruct((GROUPS, ROWS, QCOLS), bf16),
            jax.ShapeDtypeStruct((KVCOLS, GROUPS * ROWS), bf16),
        ),
        in_specs=[pl.BlockSpec(memory_space=pltpu.SMEM), vmem, vmem, anywhere, anywhere],
        out_specs=(vmem, hbm, hbm),
        scratch_shapes=[
            pltpu.VMEM((4, 1024, HEAD), bf16),
            pltpu.VMEM((4, 1024, HEAD), bf16),
            pltpu.VMEM((KVCOLS, GROUPS * ROWS), bf16),
            pltpu.SemaphoreType.DMA((4,)),
        ],
        compiler_params=pltpu.CompilerParams(vmem_limit_bytes=24 << 20),
        name="attend",
    )(lengths, mixed, blocks, keys, values)


def per_device(
    token_ids, embed_table, norm_gain, w_query, w_keyvalue, key_cache, value_cache, cache_lengths
):
    r, t = lax.axis_index("replica"), lax.axis_index("tp")
    vocab_rows = embed_table.shape[0]
    ids = token_ids.reshape(Z, XH, CORES, BATCH).transpose(2, 1, 0, 3).reshape(-1)
    columns = lax.broadcasted_iota(jnp.int32, (ids.shape[0], vocab_rows), 1)
    onehot = ((ids - r * vocab_rows)[:, None] == columns).astype(jnp.bfloat16)
    part = jnp.dot(onehot, embed_table, preferred_element_type=jnp.float32).astype(jnp.bfloat16)
    part = part.reshape(CORES, XH, Z, BATCH, FEAT)
    query_cols = w_query.reshape(8, TPS, QCOLS).transpose(1, 0, 2)
    pair_cols = w_keyvalue.reshape(8, 2, TPS, 32).transpose(2, 0, 1, 3).reshape(TPS, 8, KVCOLS)
    filler = jnp.zeros((TPS, 8, MSG - QCOLS - KVCOLS), jnp.bfloat16)
    msg = jnp.concatenate([query_cols, pair_cols, filler], axis=2)
    blocks, mixed = handoff(msg, part, norm_gain.reshape(TPS, 1, FEAT))
    lengths = lax.dynamic_slice_in_dim(cache_lengths, (t % 4) * 4, 4, 0)
    context, query_full, pair_full = attend(lengths, mixed, blocks, key_cache, value_cache)
    return (
        context,
        query_full.reshape(GROUPS * ROWS, QCOLS),
        pair_full.reshape(2, 32, GROUPS * ROWS).transpose(2, 0, 1),
    )


def solution(mesh):
    both = ("replica", "tp")
    placed = (
        P(),
        P("replica", "tp"),
        P(),
        P(both, None),
        P(both, None, None),
        P(both, None, None),
        P(both, None, None),
        P("replica"),
    )
    return jax.shard_map(
        per_device,
        mesh=mesh,
        in_specs=placed,
        out_specs=(P(both, None), P(None, "tp"), P(None, None, "tp")),
        check_vma=False,
    )
```

time: 229 us -> 84.9 us (0.37)
  the two profiles are of different devices: /device:TPU:4 before, /device:TPU:16 now
where the time goes in v1:
time: 84.9 us; the launch traced here: 84.5 us
  Pallas kernels  78.1 us (92%)
  local copies, waits for them, and re-layouts  2.8 us (3%)
  other arithmetic  1.56 us (2%)
  matrix products  1.29 us (2%)
    pallas_call x1, Pallas kernels, handoff(): pl.pallas_call(handoff_kernel, out_shape=(jax.ShapeDtypeStruct((GROUPS, B...  74.5 us
    pallas_call x1, Pallas kernels, attend(): pl.pallas_call(attend_kernel, out_shape=(jax.ShapeDtypeStruct((4, GROUP *...  3.67 us

profile of v1, /device:TPU:16, one launch (start us, length us, event | category | flops | bytes accessed | tf_op | source)
XLA Modules:
  0.0 84.5 jit_solution(9150887807334231625)
XLA Ops:
  0.6 0.0 copy-start
  0.7 0.8 dynamic_slice.3.lengths
  1.5 0.1 pad.2.clone
  1.6 0.7 broadcast_subtract_fusion
  2.3 0.1 sub.21
  2.4 0.1 sub.23
  2.4 0.7 reshape.45.gain
  3.2 0.8 reshape.39
  4.0 0.1 copy.18
  4.1 0.1 reshape.40
  4.2 0.9 %maximum_maximum_fusion.msg = bf16[16,8,384]{2,1,0:T(8,128)(2,1)S(1)} fusion(bf16[16,8,64]{2,1,0:T(8,128)(2,1)S(1)} %reshape.40, bf16[16,8,256]{2,1,0:T(8,128)(2,1)} %bitcast.18, bf16[384]{0:T(512)(128)(2,1)S(1)} %pad.2.clone), kind=kLoop, calls=%fused_computation.4 | loop fusion | flops 294912 | bytes 180992 | tf_op jit(solution)/shard_map/concatenate | solution.py:365
  5.0 0.0 copy-done
  5.1 1.3 %fusion.2 = bf16[1024,512]{1,0:T(8,128)(2,1)S(1)} fusion(bf16[1024,512]{1,0:T(8,128)(2,1)S(1)} %copy-done, s32[1024]{0:T(1024)S(1)} %sub.23), kind=kOutput, calls=%fused_computation.3 | convolution fusion | flops 1075314688 | bytes 2101248 | tf_op jit(solution)/shard_map/dot_general | solution.py:360
  6.4 0.0 copy-start.1
  6.4 0.0 copy-start.2
  6.4 74.5 %handoff.1 = (bf16[64,160,256]{2,1,0:T(8,128)(2,1)S(1)}, bf16[4,4,384]{2,1,0:T(4,128)(2,1)S(1)}) custom-call(bf16[16,8,384]{2,1,0:T(8,128)(2,1)S(1)} %maximum_maximum_fusion.msg, bf16[2,4,8,16,512]{4,3,2,1,0:T(8,128)(2,1)S(1)} %bitcast.15, bf16[16,1,512]{2,1,0:T(2,128)(2,1)S(1)} %reshape.45.gain), custom_call_target="tpu_custom_call" | custom-call | flops 17179869184 | bytes 8388608 | tf_op jit(solution)/shard_map/handoff/pallas_call | solution.py:239
  80.9 0.0 copy-done.1
  80.9 0.0 copy-done.2
  80.9 3.7 %attend.1 = (bf16[4,1024]{1,0:T(4,128)(2,1)}, bf16[64,128,256]{2,1,0:T(8,128)(2,1)}, bf16[64,8192]{1,0:T(8,128)(2,1)}) custom-call(s32[4]{0:T(128)S(1)} %dynamic_slice.3.lengths, bf16[4,4,384]{2,1,0:T(4,128)(2,1)S(1)} %get-tuple-element.8.mixed, bf16[64,160,256]{2,1,0:T(8,128)(2,1)S(1)} %get-tuple-element.9.blocks, bf16[4,1024,128]{2,1,0:T(8,128)(2,1)S(1)} %copy-done.1, ...), custom_call_target="tpu_custom_call" | custom-call | tf_op jit(solution)/shard_map/attend/pallas_call | solution.py:332
  (2 shorter events, 0.0 us)
Async XLA Ops:
  0.6 4.4 %copy-start = (bf16[1024,512]{1,0:T(8,128)(2,1)S(1)}, bf16[1024,512]{1,0:T(8,128)(2,1)}, u32[]{:S(2)}) copy-start(bf16[1024,512]{1,0:T(8,128)(2,1)} %param.9) | copy-start | bytes 3145732
  6.4 74.5 %copy-start.1 = (bf16[4,1024,128]{2,1,0:T(8,128)(2,1)S(1)}, bf16[4,1024,128]{2,1,0:T(8,128)(2,1)}, u32[]{:S(2)}) copy-start(bf16[4,1024,128]{2,1,0:T(8,128)(2,1)} %keys_hbm.1) | copy-start | bytes 3145732
  6.4 74.5 %copy-start.2 = (bf16[4,1024,128]{2,1,0:T(8,128)(2,1)S(1)}, bf16[4,1024,128]{2,1,0:T(8,128)(2,1)}, u32[]{:S(2)}) copy-start(bf16[4,1024,128]{2,1,0:T(8,128)(2,1)} %values_hbm.1) | copy-start | bytes 3145732

commit v2 on v1

v2 whole, which is shorter than its diff:
```python
import functools
import jax
import jax.numpy as jnp
from jax import lax
from jax.experimental import pallas as pl
from jax.experimental.pallas import tpu as pltpu
from jax.sharding import PartitionSpec as P

MESH = pl.DeviceIdType.MESH
Z, XH, CORES, TPS = 8, 4, 2, 16
GROUPS = Z * XH * CORES
BATCH, HEAD, GROUP, KVH = 16, 128, 8, 4
FEAT = 512
ROWS = 128
BLOCK = 160
QCOLS = 256
KVCOLS = 64
MSG = 384
PIECES = 2
PIECE = BLOCK // PIECES


def link_events():
    lag, block, token = 2.2, 1.76 / PIECES, 1.4
    ready = [(1.5, "sum", 0)]
    for j, at in ((0, 6.5), (1, 10.5), (3, 10.5), (2, 13.5)):
        ready += [(at + 1.7 * p, "block", j, p, 0) for p in range(PIECES)]
    free, events = 0.0, []
    while ready:
        ready.sort()
        at, kind, *what = ready.pop(0)
        events.append((at, kind, *what))
        if what[-1] == 4:
            continue
        if kind == "sum":
            took = token / 2 if what[-1] == 0 else token
        else:
            took = block / 2 if what[-1] == 3 else block
        free = max(free, at) + took
        ready.append((free + lag, kind, *what[:-1], what[-1] + 1))
    return events


def handoff_kernel(
    ids, gain, table_hbm, query_hbm, pair_hbm, blocks, pair, mixed,
    table, query, pairs, part, got_core, sums, up_sums, down_sums, got_x, sum_x, own_pairs, turned, embedded,
    normed, sent, acc_q, acc_kv,
    in_s, p1_s, p1_r, p2_s, p2_r, xw_s, xw_r, zp_s, zp_r, zm_s, zm_r, pf_s, pf_r, e1_s, e1_r, eu_s, eu_r, ed_s, ed_r,
    e2_s, e2_r, e4_s, e4_r, e7_s, e7_r,
):
    r, t = lax.axis_index("replica"), lax.axis_index("tp")
    z, xh, c = r // 8, (r // 2) % 4, r % 2
    f32, bf16 = jnp.float32, jnp.bfloat16

    def rep(z_, xh_, c_):
        return (z_ * XH + xh_) * CORES + c_

    def dev(rep_, tp_):
        return {"replica": rep_, "tp": tp_}

    partner = dev(rep(z, xh, 1 - c), t)

    def x_peer(d):
        return dev(rep(z, (xh + d) % XH, c), t)

    def z_peer(d):
        return dev(rep((z + d) % Z, xh, c), t)

    def t_peer(d):
        return dev(r, (t + d) % TPS)

    loads = [
        pltpu.make_async_copy(table_hbm, table, in_s.at[0]),
        pltpu.make_async_copy(query_hbm, query, in_s.at[1]),
        pltpu.make_async_copy(pair_hbm, pairs, in_s.at[2]),
    ]
    for load in loads:
        load.start()
    barrier = pltpu.get_barrier_semaphore()
    peers = [partner] + [x_peer(d) for d in (1, 2, 3)] + [z_peer(1), z_peer(Z - 1)]
    peers += [t_peer(d) for d in range(1, 16)]
    for p in peers:
        pl.semaphore_signal(barrier, inc=1, device_id=p, device_id_type=MESH)

    started = []

    def send(src, dst, ss, rs, to):
        copy = pltpu.make_async_remote_copy(
            src_ref=src, dst_ref=dst, send_sem=ss, recv_sem=rs, device_id=to, device_id_type=MESH
        )
        copy.start()
        started.append(copy)

    def arrived(dst, rs, frm):
        pltpu.make_async_remote_copy(
            src_ref=dst, dst_ref=dst, send_sem=rs, recv_sem=rs, device_id=frm, device_id_type=MESH
        ).wait_recv()

    base = r * table.shape[0]
    loads[0].wait()
    lane = lax.broadcasted_iota(jnp.int32, (128, 128), 1)

    @pl.loop(0, Z)
    def _(k):
        named = jnp.broadcast_to((ids[pl.ds(k, 1), :] - base).astype(f32), (128, 128)).T
        hot = jnp.concatenate(
            [(named == (lane + 128 * q).astype(f32)).astype(bf16) for q in range(8)], axis=1
        )
        rows = jnp.dot(hot, table[...], preferred_element_type=f32).astype(bf16)
        rows = rows.reshape(XH, CORES, BATCH, FEAT)
        part[0, k] = rows[:, 0]
        part[1, k] = rows[:, 1]

    own = rep(z, xh, c)
    first_row = pl.multiple_of(t * 8, 8)
    heads_at = pl.multiple_of((t // 4) * 128, 128)
    loads[1].wait()
    loads[2].wait()
    blocks[own, pl.ds(first_row, 8), :] = query[:, pl.ds(pl.multiple_of(t * QCOLS, QCOLS), QCOLS)]
    own_pairs[t] = pairs[:, :, pl.ds(heads_at, 128)]
    pl.semaphore_wait(barrier, len(peers))

    def turn_z(d):
        return (z + d) % Z

    core_order = (4, 3, 5, 2, 6, 1, 7, 0)
    for d in core_order:
        send(part.at[1 - c, turn_z(d)], got_core.at[turn_z(d)], e1_s.at[d], e1_r.at[d], partner)
    for d in (12, 4, 11, 5, 13, 3, 10, 6, 14, 2, 9, 7, 15, 1, 8):
        to = (t + d) % TPS
        send(
            query.at[:, pl.ds(pl.multiple_of(to * QCOLS, QCOLS), QCOLS)],
            blocks.at[own, pl.ds(first_row, 8), :],
            p1_s.at[d], p1_r.at[d], t_peer(d),
        )
        send(
            pairs.at[:, :, pl.ds(pl.multiple_of((to // 4) * 128, 128), 128)],
            own_pairs.at[t],
            p2_s.at[d], p2_r.at[d], t_peer(d),
        )

    def add_core(d):
        arrived(got_core.at[turn_z(d)], e1_r.at[d], partner)
        sums[turn_z(d)] = part[c, turn_z(d)] + got_core[turn_z(d)]

    def on_sum(step):
        up_dst, down_dst = up_sums.at[step], down_sums.at[step]
        if step == 0:
            add_core(4)
            up, down = sums.at[turn_z(4), pl.ds(0, 2)], sums.at[turn_z(4), pl.ds(2, 2)]
            up_dst, down_dst = up_dst.at[pl.ds(0, 2)], down_dst.at[pl.ds(2, 2)]
        else:
            up, down = up_sums.at[step - 1], down_sums.at[step - 1]
            up_got, down_got = up, down
            if step == 1:
                up_got, down_got = up.at[pl.ds(0, 2)], down.at[pl.ds(2, 2)]
            arrived(up_got, eu_r.at[step - 1], z_peer(Z - 1))
            arrived(down_got, ed_r.at[step - 1], z_peer(1))
            if step == 4:
                add_z()
                return
            above, below = turn_z(4 - step), turn_z(4 + step)
            if step == 1:
                up_sums[0, 0:2] = up_sums[0, 0:2] + sums[above, 0:2]
                up_sums[0, 2:4] = sums[above, 2:4]
                down_sums[0, 2:4] = down_sums[0, 2:4] + sums[below, 2:4]
                down_sums[0, 0:2] = sums[below, 0:2]
            else:
                up_sums[step - 1] = up_sums[step - 1] + sums[above]
                down_sums[step - 1] = down_sums[step - 1] + sums[below]
        send(up, up_dst, eu_s.at[step], eu_r.at[step], z_peer(1))
        send(down, down_dst, ed_s.at[step], ed_r.at[step], z_peer(Z - 1))
        if step == 0:
            for d in core_order[1:]:
                add_core(d)

    def add_z():
        sum_x[...] = (sums[z] + up_sums[3]) + down_sums[3]
        for d in (2, 1, 3):
            send(sum_x.at[(xh + d) % XH], got_x.at[d - 1], e2_s.at[d], e2_r.at[d], x_peer(d))

    def add_x():
        for d in (1, 3, 2):
            arrived(got_x.at[d - 1], e2_r.at[d], x_peer(XH - d))
        embedded[t] = (sum_x[xh] + got_x[0]) + (got_x[1] + got_x[2])
        for d in (12, 4, 11, 5, 13, 3, 10, 6, 14, 2, 9, 7, 15, 1, 8):
            send(embedded.at[t], embedded.at[t], e4_s.at[d], e4_r.at[d], t_peer(d))

    def whole_block():
        for d in range(1, 16):
            frm = (t - d + TPS) % TPS
            arrived(own_pairs.at[frm], p2_r.at[d], t_peer(TPS - d))
        even = lax.broadcasted_iota(jnp.int32, (256, 256), 1)
        even = jnp.where(even < 128, 2 * even, 2 * even - 255)
        pick = (lax.broadcasted_iota(jnp.int32, (256, 256), 0) == even).astype(bf16)
        turned[...] = lax.dot_general(
            own_pairs[...].reshape(256, 128), pick, (((0,), (0,)), ((), ())),
            preferred_element_type=f32,
        )
        mine = pl.multiple_of((t % 4) * 32, 32)
        blocks[own, ROWS:BLOCK, :] = turned[pl.ds(mine, 32), :].astype(bf16)
        for d in range(1, 16):
            frm = (t - d + TPS) % TPS
            arrived(
                blocks.at[own, pl.ds(pl.multiple_of(frm * 8, 8), 8), :], p1_r.at[d], t_peer(TPS - d)
            )

    def block_id(dz, j):
        return rep((z + dz + 2 * Z) % Z, (xh - j + XH) % XH, c)

    def mirrored(dz, j):
        return rep((z + dz + 2 * Z) % Z, (xh - j + XH) % XH, 1 - c)

    def piece(ref, p):
        return ref.at[pl.ds(p * PIECE, PIECE)]

    def to_ring(j, p, step):
        up, down = piece(blocks.at[block_id(-step, j)], p), piece(blocks.at[block_id(step, j)], p)
        if step < 3 or p == 0:
            send(up, up, zp_s.at[j, p, step], zp_r.at[j, p, step], z_peer(1))
        if step < 3 or p == 1:
            send(down, down, zm_s.at[j, p, step], zm_r.at[j, p, step], z_peer(Z - 1))

    def to_partner(ref, k, j):
        send(ref, ref, pf_s.at[j, k], pf_r.at[j, k], partner)

    def on_block(j, p, step):
        if step == 0:
            if j == 0 and p == 0:
                whole_block()
            mine = piece(blocks.at[block_id(0, j)], p)
            if j:
                arrived(mine, xw_r.at[j, p], x_peer(XH - j))
            else:
                for d in (1, 3, 2):
                    send(mine, mine, xw_s.at[d, p], xw_r.at[d, p], x_peer(d))
            to_ring(j, p, 0)
            if p == PIECES - 1:
                to_partner(blocks.at[block_id(0, j)], 0, j)
            return
        up, down = blocks.at[block_id(-step, j)], blocks.at[block_id(step, j)]
        if step < 4 or p == 0:
            arrived(piece(up, p), zp_r.at[j, p, step - 1], z_peer(Z - 1))
        if step < 4 or p == 1:
            arrived(piece(down, p), zm_r.at[j, p, step - 1], z_peer(1))
        if step < 4:
            to_ring(j, p, step)
            if p == PIECES - 1:
                to_partner(up, 2 * step - 1, j)
                to_partner(down, 2 * step, j)
        else:
            to_partner(piece(up, p), 7 + p, j)

    def from_partner(step):
        for j in range(XH):
            up, down = blocks.at[mirrored(-step, j)], blocks.at[mirrored(step, j)]
            if step == 0:
                arrived(up, pf_r.at[j, 0], partner)
            elif step < 4:
                arrived(up, pf_r.at[j, 2 * step - 1], partner)
                arrived(down, pf_r.at[j, 2 * step], partner)
            else:
                for p in range(PIECES):
                    arrived(piece(up, p), pf_r.at[j, 7 + p], partner)

    def normalize():
        for d in range(1, 16):
            arrived(embedded.at[(t - d + TPS) % TPS], e4_r.at[d], t_peer(TPS - d))

        def squares(k, total):
            v = embedded[k].astype(f32)
            return total + v * v

        squared = lax.fori_loop(0, TPS, squares, jnp.zeros((BATCH, FEAT), f32))
        mean_square = jnp.sum(squared, axis=1, keepdims=True) * (1.0 / (TPS * FEAT))
        factor = lax.rsqrt(mean_square + 1e-05)

        @pl.loop(0, TPS)
        def _(k):
            normed[k] = (embedded[k].astype(f32) * factor * gain[k].astype(f32)).astype(bf16)

        acc_q[...] = jnp.zeros_like(acc_q)
        acc_kv[...] = jnp.zeros_like(acc_kv)

    def multiply(k):
        lhs = normed[k]
        rows = [blocks[4 * k + i, 0:ROWS, :] for i in range(4)]
        acc_q[...] += jnp.dot(lhs, jnp.concatenate(rows, axis=0), preferred_element_type=f32)
        keys = [blocks[4 * k + i, ROWS:BLOCK, 0:HEAD] for i in range(4)]
        values = [blocks[4 * k + i, ROWS:BLOCK, HEAD:QCOLS] for i in range(4)]
        both = jnp.concatenate(
            [jnp.concatenate(keys, axis=1), jnp.concatenate(values, axis=1)], axis=0
        )
        acc_kv[:, 0:KVCOLS] += lax.dot_general(
            lhs, both, (((1,), (1,)), ((), ())), preferred_element_type=f32
        )

    def multiply_early():
        normalize()
        for step in range(4):
            from_partner(step)

        @pl.loop(0, 14)
        def _(k):
            multiply(2 * ((z + 5 + k // 2) % Z) + k % 2)

    events = link_events()
    last_early = max(at for at, *what in events if what[-1] < 4)
    todo = []
    for at, kind, *what in events:
        act = functools.partial(on_sum if kind == "sum" else on_block, *what)
        todo.append((at, act))
        if kind == "sum" and what[-1] == 4:
            todo += [(at + 4.5, add_x), (max(at + 13.0, last_early + 0.1), multiply_early)]
    for _, act in sorted(todo, key=lambda item: item[0]):
        act()

    from_partner(4)
    for k in range(2):
        multiply(2 * turn_z(4) + k)

    quarter = t % 4
    for i in range(4):
        sent[i, :, 0:QCOLS] = acc_q[4 * i : 4 * i + 4, :].astype(bf16)
        sent[i, :, QCOLS:MSG] = acc_kv[4 * i : 4 * i + 4, :].astype(bf16)
    mixed[quarter] = sent[quarter]
    for d in range(1, 4):
        to = (quarter + d) % 4
        send(sent.at[to], mixed.at[quarter], e7_s.at[d], e7_r.at[d], dev(r, t - quarter + to))
    for g in range(GROUPS):
        pair[0:32, g * ROWS : (g + 1) * ROWS] = blocks[g, ROWS:BLOCK, 0:HEAD]
        pair[32:64, g * ROWS : (g + 1) * ROWS] = blocks[g, ROWS:BLOCK, HEAD:QCOLS]
    for copy in started[:-3]:
        copy.wait_send()
    for d in range(1, 4):
        frm = (quarter - d + 4) % 4
        arrived(mixed.at[frm], e7_r.at[d], dev(r, t - quarter + frm))
    for copy in started[-3:]:
        copy.wait_send()


def handoff(ids, gain, table, query, pairs):
    bf16, f32 = jnp.bfloat16, jnp.float32
    vmem = pl.BlockSpec(memory_space=pltpu.VMEM)
    hbm = pl.BlockSpec(memory_space=pltpu.HBM)
    dma = pltpu.SemaphoreType.DMA
    return pl.pallas_call(
        handoff_kernel,
        out_shape=(
            jax.ShapeDtypeStruct((GROUPS, BLOCK, QCOLS), bf16),
            jax.ShapeDtypeStruct((KVCOLS, GROUPS * ROWS), bf16),
            jax.ShapeDtypeStruct((4, 4, MSG), bf16),
        ),
        in_specs=[vmem, vmem, hbm, hbm, hbm],
        out_specs=(vmem, vmem, vmem),
        scratch_shapes=[
            pltpu.VMEM(table.shape, bf16),
            pltpu.VMEM(query.shape, bf16),
            pltpu.VMEM(pairs.shape, bf16),
            pltpu.VMEM((CORES, Z, XH, BATCH, FEAT), bf16),
            pltpu.VMEM((Z, XH, BATCH, FEAT), bf16),
            pltpu.VMEM((Z, XH, BATCH, FEAT), bf16),
            pltpu.VMEM((4, XH, BATCH, FEAT), bf16),
            pltpu.VMEM((4, XH, BATCH, FEAT), bf16),
            pltpu.VMEM((3, BATCH, FEAT), bf16),
            pltpu.VMEM((XH, BATCH, FEAT), bf16),
            pltpu.VMEM((TPS, 8, 2, 128), bf16),
            pltpu.VMEM((128, 256), f32),
            pltpu.VMEM((TPS, BATCH, FEAT), bf16),
            pltpu.VMEM((TPS, BATCH, FEAT), bf16),
            pltpu.VMEM((4, 4, MSG), bf16),
            pltpu.VMEM((BATCH, QCOLS), f32),
            pltpu.VMEM((BATCH, HEAD), f32),
            dma((3,)), dma((16,)), dma((16,)), dma((16,)), dma((16,)), dma((4, 2)), dma((4, 2)),
            dma((4, 2, 4)), dma((4, 2, 4)), dma((4, 2, 4)), dma((4, 2, 4)),
            dma((4, 9)), dma((4, 9)), dma((8,)), dma((8,)), dma((4,)), dma((4,)), dma((4,)), dma((4,)),
            dma((4,)), dma((4,)), dma((16,)), dma((16,)), dma((4,)), dma((4,)),
        ],
        compiler_params=pltpu.CompilerParams(
            collective_id=0, has_side_effects=True, vmem_limit_bytes=40 << 20
        ),
        cost_estimate=pl.CostEstimate(flops=1 << 34, bytes_accessed=1 << 23, transcendentals=0),
        name="handoff",
    )(ids, gain, table, query, pairs)


def attend_kernel(
    lengths, mixed, blocks, pair, keys_hbm, values_hbm, context, query_out, pair_out, keys, values, sems
):
    copies = [
        pltpu.make_async_copy(keys_hbm, keys, sems.at[0]),
        pltpu.make_async_copy(values_hbm, values, sems.at[1]),
        pltpu.make_async_copy(blocks.at[:, 0:ROWS, :], query_out, sems.at[2]),
        pltpu.make_async_copy(pair, pair_out, sems.at[3]),
    ]
    for copy in copies:
        copy.start()

    first = (lax.axis_index("tp") % 4) * 4
    got = [mixed[j].astype(jnp.float32) for j in range(4)]
    scale = HEAD ** (-0.5)
    copies[0].wait()
    rows = []
    for r in range(4):
        heads = [got[j][r : r + 1, k * HEAD : (k + 1) * HEAD] for j in range(4) for k in range(2)]
        query32 = jnp.concatenate(heads, axis=0)
        query = query32.astype(jnp.bfloat16)
        key_new = jnp.concatenate([got[j][r : r + 1, QCOLS : QCOLS + 32] for j in range(4)], axis=1)
        value_new = jnp.concatenate(
            [got[j][r : r + 1, QCOLS + 32 : QCOLS + 64] for j in range(4)], axis=1
        )
        scores = (
            lax.dot_general(
                query, keys[r], (((1,), (1,)), ((), ())), preferred_element_type=jnp.float32
            )
            * scale
        )
        position = lax.broadcasted_iota(jnp.int32, scores.shape, 1)
        scores = jnp.where(position < lengths[first + r], scores, -jnp.inf)
        own = jnp.sum(query32 * key_new, axis=1, keepdims=True) * scale
        top = jnp.maximum(jnp.max(scores, axis=1, keepdims=True), own)
        weights = jnp.exp(scores - top)
        own_weight = jnp.exp(own - top)
        total = jnp.sum(weights, axis=1, keepdims=True) + own_weight
        weights = (weights / total).astype(jnp.bfloat16)
        own_weight = (own_weight / total).astype(jnp.bfloat16).astype(jnp.float32)
        if r == 0:
            copies[1].wait()
        found = jnp.dot(weights, values[r], preferred_element_type=jnp.float32)
        rows.append(found + own_weight * value_new)
    lanes = [jnp.concatenate([rows[r][h : h + 1] for r in range(4)], axis=0) for h in range(GROUP)]
    context[...] = jnp.concatenate(lanes, axis=1).astype(jnp.bfloat16)
    copies[2].wait()
    copies[3].wait()


def attend(lengths, mixed, blocks, pair, keys, values):
    bf16 = jnp.bfloat16
    vmem = pl.BlockSpec(memory_space=pltpu.VMEM)
    anywhere = pl.BlockSpec(memory_space=pl.ANY)
    hbm = pl.BlockSpec(memory_space=pltpu.HBM)
    return pl.pallas_call(
        attend_kernel,
        out_shape=(
            jax.ShapeDtypeStruct((4, GROUP * HEAD), bf16),
            jax.ShapeDtypeStruct((GROUPS, ROWS, QCOLS), bf16),
            jax.ShapeDtypeStruct((KVCOLS, GROUPS * ROWS), bf16),
        ),
        in_specs=[pl.BlockSpec(memory_space=pltpu.SMEM), vmem, vmem, vmem, anywhere, anywhere],
        out_specs=(vmem, hbm, hbm),
        scratch_shapes=[
            pltpu.VMEM((4, 1024, HEAD), bf16),
            pltpu.VMEM((4, 1024, HEAD), bf16),
            pltpu.SemaphoreType.DMA((4,)),
        ],
        compiler_params=pltpu.CompilerParams(vmem_limit_bytes=24 << 20),
        name="attend",
    )(lengths, mixed, blocks, pair, keys, values)


def per_device(
    token_ids, embed_table, norm_gain, w_query, w_keyvalue, key_cache, value_cache, cache_lengths
):
    blocks, pair, mixed = handoff(
        token_ids.reshape(Z, XH * CORES * BATCH),
        norm_gain.reshape(TPS, 1, FEAT),
        *(pltpu.with_memory_space_constraint(a, pltpu.HBM) for a in (embed_table, w_query, w_keyvalue)),
    )
    context, query_full, pair_full = attend(cache_lengths, mixed, blocks, pair, key_cache, value_cache)
    return (
        context,
        query_full.reshape(GROUPS * ROWS, QCOLS),
        pair_full.reshape(2, 32, GROUPS * ROWS).transpose(2, 0, 1),
    )


def solution(mesh):
    both = ("replica", "tp")
    placed = (
        P(),
        P("replica", "tp"),
        P(),
        P(both, None),
        P(both, None, None),
        P(both, None, None),
        P(both, None, None),
        P("replica"),
    )
    return jax.shard_map(
        per_device,
        mesh=mesh,
        in_specs=placed,
        out_specs=(P(both, None), P(None, "tp"), P(None, None, "tp")),
        check_vma=False,
    )
```

time: 84.9 us -> 77.2 us (0.909)
  the two profiles are of different devices: /device:TPU:16 before, /device:TPU:1 now
where the time goes in v2:
time: 77.2 us; the launch traced here: 75.8 us
  Pallas kernels  73.7 us (95%)
  local copies, waits for them, and re-layouts  1.43 us (2%)
    pallas_call x1, Pallas kernels, handoff(): pl.pallas_call(handoff_kernel, out_shape=(jax.ShapeDtypeStruct((GROUPS, B...  70 us
    pallas_call x1, Pallas kernels, attend(): pl.pallas_call(attend_kernel, out_shape=(jax.ShapeDtypeStruct((4, GROUP *...  3.67 us

profile of v2, /device:TPU:1, one launch (start us, length us, event | category | flops | bytes accessed | tf_op | source)
XLA Modules:
  0.0 75.8 jit_solution(9562445513772405096)
XLA Ops:
  0.6 0.7 reshape.22.gain
  1.4 0.0 copy-start.3
  1.4 0.7 copy-done.3
  2.0 0.0 copy-start
  2.0 0.0 copy-start.1
  2.1 0.0 copy-start.2
  2.1 70.0 %handoff.1 = (bf16[64,160,256]{2,1,0:T(8,128)(2,1)S(1)}, bf16[64,8192]{1,0:T(8,128)(2,1)S(1)}, bf16[4,4,384]{2,1,0:T(4,128)(2,1)S(1)}) custom-call(s32[8,128]{1,0:T(8,128)S(1)} %bitcast.5, bf16[16,1,512]{2,1,0:T(2,128)(2,1)S(1)} %reshape.22.gain, bf16[1024,512]{1,0:T(8,128)(2,1)} %table_hbm.1, bf16[8,4096]{1,0:T(8,128)(2,1)} %query_hbm.1, ...), custom_call_target="tpu_custom_call" | custom-call | flops 17179869184 | bytes 8388608 | tf_op jit(solution)/shard_map/handoff/pallas_call | solution.py:347
  72.1 0.0 copy-done
  72.1 0.0 copy-done.1
  72.1 0.0 copy-done.2
  72.1 3.7 %attend.1 = (bf16[4,1024]{1,0:T(4,128)(2,1)}, bf16[64,128,256]{2,1,0:T(8,128)(2,1)}, bf16[64,8192]{1,0:T(8,128)(2,1)}) custom-call(s32[16]{0:T(128)S(1)} %copy-done.2, bf16[4,4,384]{2,1,0:T(4,128)(2,1)S(1)} %get-tuple-element.9.mixed, bf16[64,160,256]{2,1,0:T(8,128)(2,1)S(1)} %get-tuple-element.10.blocks, bf16[64,8192]{1,0:T(8,128)(2,1)S(1)} %get-tuple-element.11.pair, ...), custom_call_target="tpu_custom_call" | custom-call | tf_op jit(solution)/shard_map/attend/pallas_call | solution.py:442
Async XLA Ops:
  1.4 0.7 copy-start.3
  2.0 70.1 %copy-start = (bf16[4,1024,128]{2,1,0:T(8,128)(2,1)S(1)}, bf16[4,1024,128]{2,1,0:T(8,128)(2,1)}, u32[]{:S(2)}) copy-start(bf16[4,1024,128]{2,1,0:T(8,128)(2,1)} %keys_hbm.1) | copy-start | bytes 3145732
  2.0 70.1 %copy-start.1 = (bf16[4,1024,128]{2,1,0:T(8,128)(2,1)S(1)}, bf16[4,1024,128]{2,1,0:T(8,128)(2,1)}, u32[]{:S(2)}) copy-start(bf16[4,1024,128]{2,1,0:T(8,128)(2,1)} %values_hbm.1) | copy-start | bytes 3145732
  2.1 70.1 %copy-start.2 = (s32[16]{0:T(128)S(1)}, s32[16]{0:T(128)}, u32[]{:S(2)}) copy-start(s32[16]{0:T(128)} %lengths.1) | copy-start | bytes 196

commit v3 on v2

v3 whole, which is shorter than its diff:
```python
import functools
import math
import jax
import jax.numpy as jnp
from jax import lax
from jax.experimental import pallas as pl
from jax.experimental.pallas import tpu as pltpu
from jax.sharding import PartitionSpec as P

MESH = pl.DeviceIdType.MESH
Z, XH, CORES, TPS = 8, 4, 2, 16
GROUPS = Z * XH * CORES
BATCH, HEAD, GROUP, KVH = 16, 128, 8, 4
FEAT = 512
ROWS = 128
BLOCK = 320
SLOTS = 62
QCOLS = 256
KVCOLS = 64
MSG = 384


def link_events():
    lag = 2.2
    waiting, free, events = [(1.5, "sum", 0), (6.5, "own")], {"z": 0.0, "x": 0.0}, []

    def push(link, at, took, *what):
        free[link] = max(free[link], at) + took
        waiting.append((free[link] + lag, *what))

    while waiting:
        waiting.sort(key=lambda item: item[0])
        at, kind, *what = waiting.pop(0)
        events.append((at, kind, *what))
        step = what[0] if what else 0
        if kind == "sum":
            if step < 4:
                push("z", at, 1.4 if step else 0.7, "sum", step + 1)
            else:
                push("x", at, 1.4, "x_sum")
        elif kind == "own":
            push("z", at, 0.7, "z_first", 1)
            push("x", at, 2.1, "x_first", 1)
            push("z", at, 1.06, "ring", 1, 0)
            push("x", at, 1.4, "x_last", 1, 0)
        elif kind == "z_first":
            if step < 4:
                push("z", at, 0.7 if step < 3 else 0.35, "z_first", step + 1)
            push("x", at, 2.8 if step < 4 else 1.4, "x_last", 1, step)
        elif kind == "x_first":
            if step == 1:
                push("x", at, 1.05, "x_first", 2)
            for j in (1, 3) if step == 1 else (2,):
                push("z", at, 1.06, "ring", 1, j)
        elif kind == "ring" and step < 4:
            push("z", at, 1.06 if step < 3 else 0.53, "ring", step + 1, what[1])
        elif kind == "x_last" and step == 1:
            push("x", at, 1.4 if 0 < what[1] < 4 else 0.7, "x_last", 2, what[1])
    return events


def handoff_kernel(
    ids_hbm, gain_hbm, table_hbm, query_hbm, pair_hbm, blocks, pair, mixed,
    ids, gain, table, query, pairs, part, got_core, sums, up_sums, down_sums, got_x, sum_x, own_query, own_pairs, turned, embedded,
    normed, sent, acc_q, acc_kv,
    in_s, sems,
):
    r, t = lax.axis_index("replica"), lax.axis_index("tp")
    z, xh, c = r // 8, (r // 2) % 4, r % 2
    f32, bf16 = jnp.float32, jnp.bfloat16

    def rep(z_, xh_, c_):
        return (z_ * XH + xh_) * CORES + c_

    def dev(rep_, tp_):
        return {"replica": rep_, "tp": tp_}

    partner = dev(rep(z, xh, 1 - c), t)

    def x_peer(d):
        return dev(rep(z, (xh + d) % XH, c), t)

    def z_peer(d):
        return dev(rep((z + d) % Z, xh, c), t)

    def t_peer(d):
        return dev(r, (t + d) % TPS)

    loads = [
        pltpu.make_async_copy(table_hbm, table, in_s.at[0]),
        pltpu.make_async_copy(ids_hbm, ids, in_s.at[3]),
        pltpu.make_async_copy(gain_hbm, gain, in_s.at[4]),
        pltpu.make_async_copy(query_hbm, query, in_s.at[1]),
        pltpu.make_async_copy(pair_hbm, pairs, in_s.at[2]),
    ]
    for load in loads:
        load.start()
    barrier = pltpu.get_barrier_semaphore()
    peers = [partner] + [x_peer(d) for d in (1, 2, 3)] + [z_peer(1), z_peer(Z - 1)]
    peers += [t_peer(d) for d in range(1, 16)]
    for p in peers:
        pl.semaphore_signal(barrier, inc=1, device_id=p, device_id_type=MESH)

    slots, sent_rows = {}, {}

    def slot(*name):
        return sems.at[slots.setdefault(name, len(slots))]

    def send(src, dst, to, *name):
        kind = name[0]
        sent_rows[kind] = sent_rows.get(kind, 0) + math.prod(src.shape) // 128
        pltpu.make_async_remote_copy(
            src_ref=src, dst_ref=dst, send_sem=slot("sent", kind), recv_sem=slot(*name),
            device_id=to, device_id_type=MESH,
        ).start()

    def of_rows(rows, sem):
        for high in range(BLOCK, 0, -8):
            if rows == 36 or (rows % high == 0 and rows // high <= GROUPS):
                like = blocks.at[pl.ds(0, rows // high), pl.ds(0, high)]
                like = mixed.at[pl.ds(0, 3)] if rows == 36 else like
                return pltpu.make_async_remote_copy(
                    src_ref=like, dst_ref=like, send_sem=sem, recv_sem=sem,
                    device_id=partner, device_id_type=MESH,
                )
        raise ValueError(rows)

    def arrived(rows, *name):
        of_rows(rows, slot(*name)).wait_recv()

    base = r * table.shape[0]
    loads[0].wait()
    loads[1].wait()
    loads[2].wait()
    lane = lax.broadcasted_iota(jnp.int32, (128, 128), 1)

    @pl.loop(0, Z)
    def _(k):
        named = jnp.broadcast_to((ids[pl.ds(k, 1), :] - base).astype(f32), (128, 128)).T
        hot = jnp.concatenate(
            [(named == (lane + 128 * q).astype(f32)).astype(bf16) for q in range(8)], axis=1
        )
        rows = jnp.dot(hot, table[...], preferred_element_type=f32).astype(bf16)
        rows = rows.reshape(XH, CORES, BATCH, FEAT)
        part[0, k] = rows[:, 0]
        part[1, k] = rows[:, 1]

    own = rep(z, xh, c)
    heads_at = pl.multiple_of((t // 4) * 128, 128)
    loads[3].wait()
    loads[4].wait()
    own_query[t] = query[:, pl.ds(pl.multiple_of(t * QCOLS, QCOLS), QCOLS)]
    own_pairs[t] = pairs[:, :, pl.ds(heads_at, 128)]
    pl.semaphore_wait(barrier, len(peers))

    def turn_z(d):
        return (z + d) % Z

    far_first = (12, 4, 11, 5, 13, 3, 10, 6, 14, 2, 9, 7, 15, 1, 8)
    for d in (4, 3, 5, 2, 6, 1, 7, 0):
        at = turn_z(d)
        send(part.at[1 - c, at], got_core.at[at], partner, "core", d == 4)
    for d in far_first:
        to = (t + d) % TPS
        columns_of = pl.ds(pl.multiple_of(to * QCOLS, QCOLS), QCOLS)
        heads_of = pl.ds(pl.multiple_of((to // 4) * 128, 128), 128)
        send(query.at[:, columns_of], own_query.at[t], t_peer(d), "own_query")
        send(pairs.at[:, :, heads_of], own_pairs.at[t], t_peer(d), "own_pairs")

    def add_core(d):
        sums[turn_z(d)] = part[c, turn_z(d)] + got_core[turn_z(d)]

    def on_sum(step):
        up_dst, down_dst = up_sums.at[step], down_sums.at[step]
        if step == 0:
            arrived(256, "core", True)
            add_core(4)
            up, down = sums.at[turn_z(4), pl.ds(0, 2)], sums.at[turn_z(4), pl.ds(2, 2)]
            up_dst, down_dst = up_dst.at[pl.ds(0, 2)], down_dst.at[pl.ds(2, 2)]
        else:
            up, down = up_sums.at[step - 1], down_sums.at[step - 1]
            arrived(256 if step == 1 else 512, "sum", step)
            if step == 4:
                add_z()
                return
            above, below = turn_z(4 - step), turn_z(4 + step)
            if step == 1:
                up_sums[0, 0:2] = up_sums[0, 0:2] + sums[above, 0:2]
                up_sums[0, 2:4] = sums[above, 2:4]
                down_sums[0, 2:4] = down_sums[0, 2:4] + sums[below, 2:4]
                down_sums[0, 0:2] = sums[below, 0:2]
            else:
                up_sums[step - 1] = up_sums[step - 1] + sums[above]
                down_sums[step - 1] = down_sums[step - 1] + sums[below]
        send(up, up_dst, z_peer(1), "sum", step + 1)
        send(down, down_dst, z_peer(Z - 1), "sum", step + 1)
        if step == 0:
            arrived(7 * 256, "core", False)
            for d in (3, 5, 2, 6, 1, 7, 0):
                add_core(d)

    def add_z():
        sum_x[...] = (sums[z] + up_sums[3]) + down_sums[3]
        for d in (2, 1, 3):
            send(sum_x.at[(xh + d) % XH], got_x.at[d - 1], x_peer(d), "x_sum")

    def add_x():
        arrived(3 * 64, "x_sum")
        embedded[t] = (sum_x[xh] + got_x[0]) + (got_x[1] + got_x[2])
        for d in far_first:
            send(embedded.at[t], embedded.at[t], t_peer(d), "embedded")

    def whole_block():
        arrived(15 * 16, "own_pairs")
        even = lax.broadcasted_iota(jnp.int32, (256, 256), 1)
        even = jnp.where(even < 128, 2 * even, 2 * even - 255)
        pick = (lax.broadcasted_iota(jnp.int32, (256, 256), 0) == even).astype(bf16)
        turned[...] = lax.dot_general(
            own_pairs[...].reshape(256, 128), pick, (((0,), (0,)), ((), ())),
            preferred_element_type=f32,
        )
        mine = pl.multiple_of((t % 4) * 32, 32)
        blocks[own, 256:288, :] = turned[pl.ds(mine, 32), 0:128].astype(bf16)
        blocks[own, 288:320, :] = turned[pl.ds(mine, 32), 128:256].astype(bf16)
        arrived(15 * 16, "own_query")
        blocks[own, 128:256, :] = own_query[:, :, 128:256].reshape(ROWS, 128)
        blocks[own, 0:128, :] = own_query[:, :, 0:128].reshape(ROWS, 128)

    def group_at(dz, j, core):
        return rep((z + dz + 2 * Z) % Z, (xh - j + XH) % XH, core)

    def first_part(dz, j, core=c):
        return blocks.at[group_at(dz, j, core), pl.ds(0, 128)]

    def second_part(dz, j, core=c):
        return blocks.at[group_at(dz, j, core), pl.ds(128, 192)]

    def halved(ref, k):
        size = ref.shape[0] // 2
        return ref.at[pl.ds(k * size, size)]

    def column(j):
        return columns.at[:, (xh - j + XH) % XH, c, pl.ds(0, 128)]

    columns = blocks.reshape(Z, XH, CORES, BLOCK, 128)

    def column_to_partner(j):
        send(column(j), column(j), partner, "column")

    def to_partner(ref, step):
        send(ref, ref, partner, "mirrored", step)

    def z_first_on(step):
        up, down = first_part(-step, 0), first_part(step, 0)
        if step == 3:
            up, down = halved(up, 0), halved(down, 1)
        send(up, up, z_peer(1), "z_first", step + 1)
        send(down, down, z_peer(Z - 1), "z_first", step + 1)

    def offsets(step):
        return (step, -step) if 0 < step < 4 else (step,)

    def x_last_on(step):
        for dz in offsets(step):
            ref = first_part(dz, 0)
            send(ref, ref, x_peer(1), "x_last", 1, step)
            send(ref, ref, x_peer(3), "x_last", 1, step)

    def on_z_first(step):
        arrived(128 if step == 4 else 256, "z_first", step)
        if step < 4:
            z_first_on(step)
        x_last_on(step)
        if step == 4:
            column_to_partner(0)

    def on_x_last(hop, step):
        arrived(len(offsets(step)) * 256 // hop, "x_last", hop, step)
        if hop == 1:
            for dz in offsets(step):
                left, right = halved(first_part(dz, 1), 0), halved(first_part(dz, 3), 1)
                send(left, left, x_peer(1), "x_last", 2, step)
                send(right, right, x_peer(3), "x_last", 2, step)
        if step == 4:
            for j in (1, 3) if hop == 1 else (2,):
                column_to_partner(j)

    def to_ring(j, step):
        up, down = second_part(-step, j), second_part(step, j)
        if step == 3:
            up, down = halved(up, 0), halved(down, 1)
        send(up, up, z_peer(1), "ring", step + 1, j)
        send(down, down, z_peer(Z - 1), "ring", step + 1, j)

    def on_own():
        whole_block()
        z_first_on(0)
        ref = second_part(0, 0)
        send(ref, ref, x_peer(1), "x_first", 1)
        send(ref, ref, x_peer(3), "x_first", 1)
        to_ring(0, 0)
        x_last_on(0)
        to_partner(ref, 0)

    def on_x_first(hop):
        arrived(384 // hop, "x_first", hop)
        if hop == 1:
            left, right = halved(second_part(0, 1), 0), halved(second_part(0, 3), 1)
            send(left, left, x_peer(1), "x_first", 2)
            send(right, right, x_peer(3), "x_first", 2)
        for j in (1, 3) if hop == 1 else (2,):
            to_ring(j, 0)
            to_partner(second_part(0, j), 0)

    def on_ring(step, j):
        arrived(192 if step == 4 else 384, "ring", step, j)
        if step < 4:
            to_ring(j, step)
        up, down = second_part(-step, j), second_part(step, j)
        if step == 4:
            up, down = halved(up, 0), halved(down, 1)
        to_partner(up, step)
        to_partner(down, step)

    def from_partner(step):
        arrived(1536 if 0 < step < 4 else 768, "mirrored", step)

    def normalize():
        arrived(15 * 64, "embedded")

        def squares(k, total):
            v = embedded[k].astype(f32)
            return total + v * v

        squared = lax.fori_loop(0, TPS, squares, jnp.zeros((BATCH, FEAT), f32))
        mean_square = jnp.sum(squared, axis=1, keepdims=True) * (1.0 / (TPS * FEAT))
        factor = lax.rsqrt(mean_square + 1e-05)

        @pl.loop(0, TPS)
        def _(k):
            at_k = gain[pl.ds(pl.multiple_of(k * FEAT, FEAT), FEAT)]
            normed[k] = (embedded[k].astype(f32) * factor * at_k.astype(f32).reshape(1, FEAT)).astype(bf16)

    def matching(zz):
        return jnp.concatenate([normed[2 * zz], normed[2 * zz + 1]], axis=1)

    def multiply_second(offsets_z):
        q, kv = jnp.zeros((BATCH, 128), f32), jnp.zeros((BATCH, KVCOLS), f32)
        for zz in (turn_z(d) for d in offsets_z):
            lhs = matching(zz)
            rows = [blocks[8 * zz + i, 128:256, :] for i in range(8)]
            q += jnp.dot(lhs, jnp.concatenate(rows, axis=0), preferred_element_type=f32)
            both = jnp.concatenate([blocks[8 * zz + i, 256:320, :] for i in range(8)], axis=1)
            kv += lax.dot_general(
                lhs, both, (((1,), (1,)), ((), ())), preferred_element_type=f32
            )
        return q, kv

    def multiply_first(offsets_z):
        q = jnp.zeros((BATCH, 128), f32)
        for zz in (turn_z(d) for d in offsets_z):
            rows = [blocks[8 * zz + i, 0:128, :] for i in range(8)]
            q += jnp.dot(matching(zz), jnp.concatenate(rows, axis=0), preferred_element_type=f32)
        return q

    def multiply_early():
        normalize()
        for step in range(4):
            from_partner(step)
        acc_q[:, 128:256], acc_kv[:, 0:KVCOLS] = multiply_second((0, 1, 7, 2, 6, 3, 5))

    kinds = {
        "sum": on_sum, "own": on_own, "z_first": on_z_first, "x_first": on_x_first, "ring": on_ring,
        "x_last": on_x_last, "x_sum": add_x,
    }
    events = link_events()
    def order(kind, what):
        late = [("ring", 3, 2), ("x_last", 1, 4), ("early",), ("x_last", 2, 3), ("x_last", 2, 4), ("ring", 4, 2)]
        return late.index((kind, *what)) if (kind, *what) in late else -1

    todo = [(order(kind, what), at, functools.partial(kinds[kind], *what)) for at, kind, *what in events]
    todo.append((order("early", ()), 0.0, multiply_early))
    for *_, act in sorted(todo, key=lambda item: item[:2]):
        act()

    arrived(4096, "column")
    acc_q[:, 0:128] = multiply_first(range(Z))
    from_partner(4)
    q, kv = multiply_second((4,))
    acc_q[:, 128:256] += q
    acc_kv[:, 0:KVCOLS] += kv

    acc_kv[:, KVCOLS:128] = jnp.zeros((BATCH, 128 - KVCOLS), f32)
    quarter = t % 4
    for i in range(4):
        sent[i, :, 0:QCOLS] = acc_q[4 * i : 4 * i + 4, :].astype(bf16)
        sent[i, :, QCOLS:MSG] = acc_kv[4 * i : 4 * i + 4, :].astype(bf16)
    mixed[quarter] = sent[quarter]
    for d in range(1, 4):
        to = (quarter + d) % 4
        send(sent.at[to], mixed.at[quarter], dev(r, t - quarter + to), "mixed")
    for g in range(GROUPS):
        pair[:, g * ROWS : (g + 1) * ROWS] = blocks[g, 256:320, :]
    for kind, rows in sent_rows.items():
        if kind != "mixed":
            of_rows(rows, slot("sent", kind)).wait_send()
    arrived(sent_rows["mixed"], "mixed")
    of_rows(sent_rows["mixed"], slot("sent", "mixed")).wait_send()
    assert len(slots) == SLOTS, len(slots)


def handoff(ids, gain, table, query, pairs):
    bf16, f32 = jnp.bfloat16, jnp.float32
    vmem = pl.BlockSpec(memory_space=pltpu.VMEM)
    hbm = pl.BlockSpec(memory_space=pltpu.HBM)
    dma = pltpu.SemaphoreType.DMA
    return pl.pallas_call(
        handoff_kernel,
        out_shape=(
            jax.ShapeDtypeStruct((GROUPS, BLOCK, 128), bf16),
            jax.ShapeDtypeStruct((KVCOLS, GROUPS * ROWS), bf16),
            jax.ShapeDtypeStruct((4, 4, MSG), bf16),
        ),
        in_specs=[hbm] * 5,
        out_specs=(vmem, vmem, vmem),
        scratch_shapes=[
            pltpu.VMEM(ids.shape, jnp.int32),
            pltpu.VMEM(gain.shape, bf16),
            pltpu.VMEM(table.shape, bf16),
            pltpu.VMEM(query.shape, bf16),
            pltpu.VMEM(pairs.shape, bf16),
            pltpu.VMEM((CORES, Z, XH, BATCH, FEAT), bf16),
            pltpu.VMEM((Z, XH, BATCH, FEAT), bf16),
            pltpu.VMEM((Z, XH, BATCH, FEAT), bf16),
            pltpu.VMEM((4, XH, BATCH, FEAT), bf16),
            pltpu.VMEM((4, XH, BATCH, FEAT), bf16),
            pltpu.VMEM((3, BATCH, FEAT), bf16),
            pltpu.VMEM((XH, BATCH, FEAT), bf16),
            pltpu.VMEM((TPS, 8, QCOLS), bf16),
            pltpu.VMEM((TPS, 8, 2, 128), bf16),
            pltpu.VMEM((128, 256), f32),
            pltpu.VMEM((TPS, BATCH, FEAT), bf16),
            pltpu.VMEM((TPS, BATCH, FEAT), bf16),
            pltpu.VMEM((4, 4, MSG), bf16),
            pltpu.VMEM((BATCH, QCOLS), f32),
            pltpu.VMEM((BATCH, HEAD), f32),
            dma((5,)), dma((SLOTS,)),
        ],
        compiler_params=pltpu.CompilerParams(
            collective_id=0, has_side_effects=True, vmem_limit_bytes=40 << 20
        ),
        cost_estimate=pl.CostEstimate(flops=1 << 34, bytes_accessed=1 << 23, transcendentals=0),
        name="handoff",
    )(ids, gain, table, query, pairs)


def attend_kernel(
    lengths, mixed, blocks, pair, keys, values, context, query_out, pair_out, sems
):
    copies = [
        pltpu.make_async_copy(blocks.at[:, 0:128], query_out.at[:, :, 0:128], sems.at[0]),
        pltpu.make_async_copy(blocks.at[:, 128:256], query_out.at[:, :, 128:256], sems.at[1]),
        pltpu.make_async_copy(pair, pair_out, sems.at[2]),
    ]
    for copy in copies:
        copy.start()

    first = (lax.axis_index("tp") % 4) * 4
    got = [mixed[j].astype(jnp.float32) for j in range(4)]
    scale = HEAD ** (-0.5)
    queries, own, scores, lens, new_values = [], [], [], [], []
    for r in range(4):
        heads = [got[j][r : r + 1, k * HEAD : (k + 1) * HEAD] for j in range(4) for k in range(2)]
        query32 = jnp.concatenate(heads, axis=0)
        query = query32.astype(jnp.bfloat16)
        key_new = jnp.concatenate([got[j][r : r + 1, QCOLS : QCOLS + 32] for j in range(4)], axis=1)
        new_values.append(
            jnp.concatenate([got[j][r : r + 1, QCOLS + 32 : QCOLS + 64] for j in range(4)], axis=1)
        )
        scores.append(
            lax.dot_general(
                query, keys[r], (((1,), (1,)), ((), ())), preferred_element_type=jnp.float32
            )
        )
        own.append(jnp.sum(query32 * key_new, axis=1, keepdims=True) * scale)
        lens.append(jnp.full((GROUP, 1), lengths[first + r], jnp.int32))
    scores = jnp.concatenate(scores, axis=0) * scale
    own, lens = jnp.concatenate(own, axis=0), jnp.concatenate(lens, axis=0)
    position = lax.broadcasted_iota(jnp.int32, scores.shape, 1)
    scores = jnp.where(position < lens, scores, -jnp.inf)
    top = jnp.maximum(jnp.max(scores, axis=1, keepdims=True), own)
    weights = jnp.exp(scores - top)
    own_weight = jnp.exp(own - top)
    total = jnp.sum(weights, axis=1, keepdims=True) + own_weight
    weights = (weights / total).astype(jnp.bfloat16)
    own_weight = (own_weight / total).astype(jnp.bfloat16).astype(jnp.float32)
    rows = []
    for r in range(4):
        mine = slice(r * GROUP, (r + 1) * GROUP)
        found = jnp.dot(weights[mine], values[r], preferred_element_type=jnp.float32)
        rows.append(found + own_weight[mine] * new_values[r])
    lanes = [jnp.concatenate([rows[r][h : h + 1] for r in range(4)], axis=0) for h in range(GROUP)]
    context[...] = jnp.concatenate(lanes, axis=1).astype(jnp.bfloat16)
    for copy in copies:
        copy.wait()


def attend(lengths, mixed, blocks, pair, keys, values):
    bf16 = jnp.bfloat16
    vmem = pl.BlockSpec(memory_space=pltpu.VMEM)
    hbm = pl.BlockSpec(memory_space=pltpu.HBM)
    return pl.pallas_call(
        attend_kernel,
        out_shape=(
            jax.ShapeDtypeStruct((4, GROUP * HEAD), bf16),
            jax.ShapeDtypeStruct((GROUPS, ROWS, QCOLS), bf16),
            jax.ShapeDtypeStruct((KVCOLS, GROUPS * ROWS), bf16),
        ),
        in_specs=[pl.BlockSpec(memory_space=pltpu.SMEM), vmem, vmem, vmem, vmem, vmem],
        out_specs=(vmem, hbm, hbm),
        scratch_shapes=[
            pltpu.SemaphoreType.DMA((3,)),
        ],
        compiler_params=pltpu.CompilerParams(vmem_limit_bytes=24 << 20),
        name="attend",
    )(lengths, mixed, blocks, pair, keys, values)


def per_device(
    token_ids, embed_table, norm_gain, w_query, w_keyvalue, key_cache, value_cache, cache_lengths
):
    blocks, pair, mixed = handoff(
        *(
            pltpu.with_memory_space_constraint(a, pltpu.HBM)
            for a in (
                token_ids.reshape(Z, XH * CORES * BATCH), norm_gain, embed_table, w_query, w_keyvalue
            )
        ),
    )
    context, query_full, pair_full = attend(cache_lengths, mixed, blocks, pair, key_cache, value_cache)
    return (
        context,
        query_full.reshape(GROUPS * ROWS, QCOLS),
        pair_full.reshape(2, 32, GROUPS * ROWS).transpose(2, 0, 1),
    )


def solution(mesh):
    both = ("replica", "tp")
    placed = (
        P(),
        P("replica", "tp"),
        P(),
        P(both, None),
        P(both, None, None),
        P(both, None, None),
        P(both, None, None),
        P("replica"),
    )
    return jax.shard_map(
        per_device,
        mesh=mesh,
        in_specs=placed,
        out_specs=(P(both, None), P(None, "tp"), P(None, None, "tp")),
        check_vma=False,
    )
```

time: 77.2 us -> 69.2 us (0.90); the launches traced: 75.8 us -> 69.1 us
  Pallas kernels: 73.7 us -> 68.4 us
  local copies, waits for them, and re-layouts: 1.43 us -> 0.01 us
    pallas_call x1, Pallas kernels: 70 us -> 64.8 us  [handoff(): pl.pallas_call(handoff_kernel, out_shape=(jax.ShapeDtypeStruct((GROUPS, B...]
where the time goes in v3:
time: 69.2 us; the launch traced here: 69.1 us
  Pallas kernels  68.4 us (99%)
    pallas_call x1, Pallas kernels, handoff(): pl.pallas_call(handoff_kernel, out_shape=(jax.ShapeDtypeStruct((GROUPS, B...  64.8 us
    pallas_call x1, Pallas kernels, attend(): pl.pallas_call(attend_kernel, out_shape=(jax.ShapeDtypeStruct((4, GROUP *...  3.52 us

profile of v3, /device:TPU:1, one launch (start us, length us, event | category | flops | bytes accessed | tf_op | source)
XLA Modules:
  0.0 69.1 jit_solution(8332005062390922870)
XLA Ops:
  0.6 0.0 copy-start
  0.6 0.0 copy-start.1
  0.7 0.0 copy-start.2
  0.7 64.8 %handoff.1 = (bf16[64,320,128]{2,1,0:T(8,128)(2,1)S(1)}, bf16[64,8192]{1,0:T(8,128)(2,1)S(1)}, bf16[4,4,384]{2,1,0:T(4,128)(2,1)S(1)}) custom-call(s32[8,128]{1,0:T(8,128)} %bitcast.7, bf16[8192]{0:T(1024)(128)(2,1)} %gain_hbm.1, bf16[1024,512]{1,0:T(8,128)(2,1)} %table_hbm.1, bf16[8,4096]{1,0:T(8,128)(2,1)} %query_hbm.1, bf16[8,2,512]{2,1,0:T(2,128)(2,1)} %pair_hbm.1), custom_call_target="tpu_custom_call" | custom-call | flops 17179869184 | bytes 8388608 | tf_op jit(solution)/shard_map/handoff/pallas_call | solution.py:417
  65.5 0.0 copy-done
  65.5 0.0 copy-done.1
  65.5 0.0 copy-done.2
  65.5 3.5 %attend.1 = (bf16[4,1024]{1,0:T(4,128)(2,1)}, bf16[64,128,256]{2,1,0:T(8,128)(2,1)}, bf16[64,8192]{1,0:T(8,128)(2,1)}) custom-call(s32[16]{0:T(128)S(1)} %copy-done.2, bf16[4,4,384]{2,1,0:T(4,128)(2,1)S(1)} %get-tuple-element.9.mixed, bf16[64,320,128]{2,1,0:T(8,128)(2,1)S(1)} %get-tuple-element.10.blocks, bf16[64,8192]{1,0:T(8,128)(2,1)S(1)} %get-tuple-element.11.pair, ...), custom_call_target="tpu_custom_call" | custom-call | tf_op jit(solution)/shard_map/attend/pallas_call | solution.py:512
Async XLA Ops:
  0.6 64.9 %copy-start = (bf16[4,1024,128]{2,1,0:T(8,128)(2,1)S(1)}, bf16[4,1024,128]{2,1,0:T(8,128)(2,1)}, u32[]{:S(2)}) copy-start(bf16[4,1024,128]{2,1,0:T(8,128)(2,1)} %keys.1) | copy-start | bytes 3145732
  0.6 64.9 %copy-start.1 = (bf16[4,1024,128]{2,1,0:T(8,128)(2,1)S(1)}, bf16[4,1024,128]{2,1,0:T(8,128)(2,1)}, u32[]{:S(2)}) copy-start(bf16[4,1024,128]{2,1,0:T(8,128)(2,1)} %values.1) | copy-start | bytes 3145732
  0.7 64.9 %copy-start.2 = (s32[16]{0:T(128)S(1)}, s32[16]{0:T(128)}, u32[]{:S(2)}) copy-start(s32[16]{0:T(128)} %lengths.1) | copy-start | bytes 196

commit v4 on v3

--- a/solution.py
+++ b/solution.py
@@ -21,12 +21,12 @@
 
 
 def link_events():
-    lag = 2.2
+    lag = {"z": 3.2, "x": 2.2}
     waiting, free, events = [(1.5, "sum", 0), (6.5, "own")], {"z": 0.0, "x": 0.0}, []
 
     def push(link, at, took, *what):
         free[link] = max(free[link], at) + took
-        waiting.append((free[link] + lag, *what))
+        waiting.append((free[link] + lag[link], *what))
 
     while waiting:
         waiting.sort(key=lambda item: item[0])
@@ -458,9 +458,19 @@
     lengths, mixed, blocks, pair, keys, values, context, query_out, pair_out, sems
 ):
     copies = [
-        pltpu.make_async_copy(blocks.at[:, 0:128], query_out.at[:, :, 0:128], sems.at[0]),
-        pltpu.make_async_copy(blocks.at[:, 128:256], query_out.at[:, :, 128:256], sems.at[1]),
-        pltpu.make_async_copy(pair, pair_out, sems.at[2]),
+        pltpu.make_async_copy(
+            blocks.at[pl.ds(16 * k, 16), pl.ds(128 * half, 128)],
+            query_out.at[pl.ds(16 * k, 16), :, pl.ds(128 * half, 128)],
+            sems.at[2 * k + half],
+        )
+        for k in range(4)
+        for half in range(2)
+    ]
+    copies += [
+        pltpu.make_async_copy(
+            pair.at[pl.ds(32 * k, 32)], pair_out.at[pl.ds(32 * k, 32)], sems.at[8 + k]
+        )
+        for k in range(2)
     ]
     for copy in copies:
         copy.start()
@@ -519,7 +529,7 @@
         in_specs=[pl.BlockSpec(memory_space=pltpu.SMEM), vmem, vmem, vmem, vmem, vmem],
         out_specs=(vmem, hbm, hbm),
         scratch_shapes=[
-            pltpu.SemaphoreType.DMA((3,)),
+            pltpu.SemaphoreType.DMA((10,)),
         ],
         compiler_params=pltpu.CompilerParams(vmem_limit_bytes=24 << 20),
         name="attend",

time: 69.2 us -> 69.6 us (level)
  no operation moved by 1% of the time
where the time goes in v4:
time: 69.6 us; the launch traced here: 69.4 us
  Pallas kernels  68.7 us (99%)
    pallas_call x1, Pallas kernels, handoff(): pl.pallas_call(handoff_kernel, out_shape=(jax.ShapeDtypeStruct((GROUPS, B...  65.2 us
    pallas_call x1, Pallas kernels, attend(): pl.pallas_call(attend_kernel, out_shape=(jax.ShapeDtypeStruct((4, GROUP *...  3.56 us

profile of v4, /device:TPU:1, one launch (start us, length us, event | category | flops | bytes accessed | tf_op | source)
XLA Modules:
  0.0 69.4 jit_solution(6782929448774677192)
XLA Ops:
  0.6 0.0 copy-start
  0.6 0.0 copy-start.1
  0.7 0.0 copy-start.2
  0.7 65.2 %handoff.1 = (bf16[64,320,128]{2,1,0:T(8,128)(2,1)S(1)}, bf16[64,8192]{1,0:T(8,128)(2,1)S(1)}, bf16[4,4,384]{2,1,0:T(4,128)(2,1)S(1)}) custom-call(s32[8,128]{1,0:T(8,128)} %bitcast.7, bf16[8192]{0:T(1024)(128)(2,1)} %gain_hbm.1, bf16[1024,512]{1,0:T(8,128)(2,1)} %table_hbm.1, bf16[8,4096]{1,0:T(8,128)(2,1)} %query_hbm.1, bf16[8,2,512]{2,1,0:T(2,128)(2,1)} %pair_hbm.1), custom_call_target="tpu_custom_call" | custom-call | flops 17179869184 | bytes 8388608 | tf_op jit(solution)/shard_map/handoff/pallas_call | solution.py:417
  65.8 0.0 copy-done
  65.8 0.0 copy-done.1
  65.8 0.0 copy-done.2
  65.9 3.6 %attend.1 = (bf16[4,1024]{1,0:T(4,128)(2,1)}, bf16[64,128,256]{2,1,0:T(8,128)(2,1)}, bf16[64,8192]{1,0:T(8,128)(2,1)}) custom-call(s32[16]{0:T(128)S(1)} %copy-done.2, bf16[4,4,384]{2,1,0:T(4,128)(2,1)S(1)} %get-tuple-element.9.mixed, bf16[64,320,128]{2,1,0:T(8,128)(2,1)S(1)} %get-tuple-element.10.blocks, bf16[64,8192]{1,0:T(8,128)(2,1)S(1)} %get-tuple-element.11.pair, ...), custom_call_target="tpu_custom_call" | custom-call | tf_op jit(solution)/shard_map/attend/pallas_call | solution.py:522
Async XLA Ops:
  0.6 65.2 %copy-start = (bf16[4,1024,128]{2,1,0:T(8,128)(2,1)S(1)}, bf16[4,1024,128]{2,1,0:T(8,128)(2,1)}, u32[]{:S(2)}) copy-start(bf16[4,1024,128]{2,1,0:T(8,128)(2,1)} %keys.1) | copy-start | bytes 3145732
  0.6 65.2 %copy-start.1 = (bf16[4,1024,128]{2,1,0:T(8,128)(2,1)S(1)}, bf16[4,1024,128]{2,1,0:T(8,128)(2,1)}, u32[]{:S(2)}) copy-start(bf16[4,1024,128]{2,1,0:T(8,128)(2,1)} %values.1) | copy-start | bytes 3145732
  0.7 65.2 %copy-start.2 = (s32[16]{0:T(128)S(1)}, s32[16]{0:T(128)}, u32[]{:S(2)}) copy-start(s32[16]{0:T(128)} %lengths.1) | copy-start | bytes 196
